TPU v7x, 32 devices: a whole 2x2x4 slice. The times are simulated.
32 devices in a mesh: rows: 8 (over y, x, core), cols: 4 (over z).
Axes of the slice: x: 2, y: 2, z: 4, core: 2. Of those that a mesh axis runs over, the one named last changes fastest.
Arguments:
- fmap1: bfloat16 [2, 256, 256, 256], P(None, 'rows', 'cols'), may hold values from -6 to 6
- fmap2: bfloat16 [2, 256, 256, 256], P(None, 'rows', 'cols'), may hold values from -6 to 6
- target_owner: int32 [2, 2048, 1], P(None, ('rows', 'cols')), may hold values from 0 to 31; in each aligned block of 64 rows (0 to 63, 64 to 127, ..., all dimensions but the last counted through in order) at most 4 rows name the same one
- target_tile: int32 [2, 2048], P(None, ('rows', 'cols')), may hold values from 0 to 31
Outputs:
- corr: float32 [2, 81, 131072], P(None, None, ('rows', 'cols'))
Inputs may be any that keep to these rules, and one draw needn't show every extreme that they name: `target_owner`: at each level, the 64 query blocks of one region (aligned blocks of rows) name any one owner at most 4 times, a bound that some block reaches. `target_tile`: tile of the owner's region in the query block's frame, numbered row-major; level l uses it modulo that level's tile count.
All inputs are finite; a program needn't handle non-finite values.
Results may differ from a plain program's by a relative error of at most 0.0013.
Values may be sent and summed in bfloat16 or wider, within the bound.
A program may use at most 128 MiB of HBM per device.

v0:
```python
import functools

import jax
import jax.numpy as jnp
from jax import lax
from jax.experimental import pallas as pl
from jax.experimental.pallas import tpu as pltpu
from jax.sharding import PartitionSpec as P

RADIUS = 4
LEVELS = 2
STEP_SLOTS = 16


def padded_2(block, sides, width):
    for axis, dim in sides:
        count = lax.axis_size(axis)
        forward = [(i, i + 1) for i in range(count - 1)]
        backward = [(target, source) for source, target in forward]
        low = lax.ppermute(
            lax.slice_in_dim(block, block.shape[dim] - width, None, axis=dim), axis, forward
        )
        high = lax.ppermute(lax.slice_in_dim(block, 0, width, axis=dim), axis, backward)
        block = jnp.concatenate([low, block, high], axis=dim)
    return block


def pool_level(level_map):
    frame_count, rows_in, cols_in, channels = level_map.shape
    pooled = level_map.astype(jnp.float32).reshape(
        frame_count, rows_in // 2, 2, cols_in // 2, 2, channels
    )
    return jnp.mean(pooled, axis=(2, 4)).astype(jnp.bfloat16)


def dispatch_kernel(slot_count, block_ref, query_ref, sent_ref):
    base = pl.program_id(0) * slot_count
    for slot in range(slot_count):
        sent_ref[slot] = query_ref[block_ref[base + slot]]


def correlate_kernel(plan, scale, label_ref, query_ref, map_ref, reply_ref):
    per_frame, col_count, padded_rows, across = plan
    tile_side = 2 * RADIUS
    span_side = 4 * RADIUS
    window_side = 2 * RADIUS + 1
    block_cells = tile_side * tile_side
    base = pl.program_id(0) * STEP_SLOTS
    lane = lax.broadcasted_iota(jnp.int32, (1, 1, 2 * block_cells), 2)
    query_row = lane % block_cells // tile_side
    query_col = lane[0] % tile_side
    is_first = lane[0] < block_cells

    def window(slot):
        label = label_ref[base + slot]
        tile = label % per_frame
        region = label // per_frame
        row = region // col_count * padded_rows + tile // across * tile_side
        col = (region % col_count * across + tile % across) * tile_side
        col = pl.multiple_of(col, tile_side)
        cells = map_ref[pl.ds(row, span_side), pl.ds(col, span_side), :]
        return cells.reshape(span_side * span_side, -1).astype(jnp.bfloat16)

    for pair in range(STEP_SLOTS // 2):
        queries = query_ref[2 * pair : 2 * pair + 2].reshape(2 * block_cells, -1)
        first, second = [
            lax.dot_general(
                window(2 * pair + half),
                queries,
                (((1,), (1,)), ((), ())),
                preferred_element_type=jnp.float32,
            )
            for half in range(2)
        ]
        scores = jnp.where(is_first, first, second)
        scores = scores.reshape(span_side, span_side, 2 * block_cells)
        for bit in (1, 2, 4):
            scores = jnp.where((query_row & bit) != 0, scores[bit:], scores[:-bit])
        flat = scores.reshape(window_side * span_side, 2 * block_cells)
        for bit in (1, 2, 4):
            moved = pltpu.roll(flat, flat.shape[0] - bit, 0)
            flat = jnp.where((query_col & bit) != 0, moved, flat)
        flat = flat * scale
        for a in range(window_side):
            at = (pair * window_side + a) * window_side
            reply_ref[at : at + window_side, :] = flat[
                a * span_side : a * span_side + window_side
            ]


def assemble_kernel(pair_count, source_ref, half_ref, *refs):
    reply_refs, out_ref = refs[:-1], refs[-1]
    window_cells, lanes = out_ref.shape[1], reply_refs[0].shape[1]
    is_first = lax.broadcasted_iota(jnp.int32, (window_cells, lanes), 1) < lanes // 2
    for level in range(LEVELS):

        def step(m, carry, level=level):
            at = 2 * (level * pair_count + m)
            picked = []
            for side in range(2):
                first_row = source_ref[at + side] * window_cells
                rows = reply_refs[level][pl.ds(first_row, window_cells), :]
                moved = pltpu.roll(rows, lanes // 2, 1)
                picked.append(jnp.where(half_ref[at + side] == side, rows, moved))
            spot = pl.ds(pl.multiple_of(m * lanes, lanes), lanes)
            out_ref[level, :, spot] = jnp.where(is_first, picked[0], picked[1])
            return carry

        lax.fori_loop(0, pair_count, step, 0)


def body(fmap1, fmap2, target_owner, target_tile):
    tile_side = 2 * RADIUS
    window_side = 2 * RADIUS + 1
    block_cells = tile_side * tile_side
    frame_count, band_rows, band_cols, channels = fmap1.shape
    row_count = lax.axis_size("rows")
    col_count = lax.axis_size("cols")
    device_count = row_count * col_count
    tiles_across = band_cols // tile_side
    per_frame = band_rows // tile_side * tiles_across
    block_count = frame_count * per_frame
    owner_slots = max(2, (2 * block_count + device_count - 1) // device_count)
    row_slots = -(-owner_slots * col_count // STEP_SLOTS) * STEP_SLOTS
    pair_slots = row_slots // 2
    queries = fmap1.reshape(
        frame_count, band_rows // tile_side, tile_side, tiles_across, tile_side, channels
    )
    queries = queries.transpose(0, 1, 3, 2, 4, 5).reshape(block_count, block_cells, channels)
    owner_ids = target_owner[:, :, 0]
    owner_rows = owner_ids // col_count
    peer_ids = jnp.arange(row_count, dtype=jnp.int32)
    owner_hits = (owner_rows[:, :, None] == peer_ids[None, None, :]).astype(jnp.int32)
    slot_rank = jnp.sum(owner_hits * (jnp.cumsum(owner_hits, axis=1) - 1), axis=2)
    block_ids = jnp.arange(block_count, dtype=jnp.int32)
    label_rows = []
    for level in range(LEVELS):
        tile_count = (band_rows >> level) // tile_side * ((band_cols >> level) // tile_side)
        regions = block_ids // per_frame * col_count + owner_ids[level] % col_count
        label_rows.append(regions * per_frame + target_tile[level] % tile_count)
    rank_ids = jnp.arange(row_slots, dtype=jnp.int32)
    rank_hits = (slot_rank[:, :, None] == rank_ids[None, None, :]).astype(jnp.int32)
    slot_hits = owner_hits[:, :, :, None] * rank_hits[:, :, None, :]

    def by_slot(values):
        table = jnp.sum(slot_hits * values[:, :, None, None], axis=1)
        return table.transpose(1, 0, 2)

    labels_sent = by_slot(jnp.stack(label_rows))
    blocks_sent = by_slot(jnp.broadcast_to(block_ids[None], owner_ids.shape))
    slot_block = (row_slots, block_cells, channels)
    slot_total = row_count * row_slots
    label_part = lax.all_to_all(labels_sent, "rows", split_axis=0, concat_axis=0, tiled=True)
    levels = [fmap2]
    for level in range(1, LEVELS):
        levels.append(pool_level(levels[-1]))
    window_cells = window_side * window_side
    step_block = (STEP_SLOTS, block_cells, channels)
    reply_block = (STEP_SLOTS // 2 * window_cells, 2 * block_cells)
    reply_tables = [None] * LEVELS
    earlier = None
    for level in reversed(range(LEVELS)):
        queries_sent = pl.pallas_call(
            functools.partial(dispatch_kernel, row_slots),
            out_shape=jax.ShapeDtypeStruct((slot_total,) + slot_block[1:], jnp.bfloat16),
            grid_spec=pltpu.PrefetchScalarGridSpec(
                num_scalar_prefetch=1,
                grid=(row_count,),
                in_specs=[pl.BlockSpec(queries.shape, lambda d, *_: (0, 0, 0))],
                out_specs=pl.BlockSpec(slot_block, lambda d, *_: (d, 0, 0)),
            ),
        )(blocks_sent[:, level].reshape(-1), queries)
        query_part = lax.all_to_all(
            queries_sent.reshape((row_count,) + slot_block),
            "rows",
            split_axis=0,
            concat_axis=0,
            tiled=True,
        )
        band = lax.all_gather(levels[level], "cols", axis=2, tiled=True)
        if earlier is not None:
            band = lax.optimization_barrier((band, earlier, query_part))[0]
        padded = padded_2(band, (("rows", 1),), RADIUS).astype(jnp.float32)
        padded = jnp.pad(padded, ((0, 0), (0, 0), (RADIUS, RADIUS), (0, 0)))
        level_map = padded.reshape((-1,) + padded.shape[2:])
        plan = (per_frame, col_count, padded.shape[1], levels[level].shape[2] // tile_side)
        replies = pl.pallas_call(
            functools.partial(correlate_kernel, plan, channels ** (-0.5)),
            out_shape=jax.ShapeDtypeStruct(
                (row_count * pair_slots * window_cells, 2 * block_cells), jnp.float32
            ),
            grid_spec=pltpu.PrefetchScalarGridSpec(
                num_scalar_prefetch=1,
                grid=(slot_total // STEP_SLOTS,),
                in_specs=[
                    pl.BlockSpec(step_block, lambda d, *_: (d, 0, 0)),
                    pl.BlockSpec(
                        level_map.shape, lambda d, *_: (0, 0, 0), pipeline_mode=pl.Buffered(1)
                    ),
                ],
                out_specs=pl.BlockSpec(reply_block, lambda d, *_: (d, 0)),
            ),
        )(
            label_part[:, level].reshape(-1),
            query_part.reshape((slot_total,) + slot_block[1:]),
            level_map,
        )
        returned = lax.all_to_all(
            replies.reshape(row_count, pair_slots * window_cells, 2 * block_cells),
            "rows",
            split_axis=0,
            concat_axis=0,
            tiled=True,
        )
        earlier = returned
        reply_tables[level] = returned.reshape(-1, 2 * block_cells)
    source_ids = owner_rows * pair_slots + slot_rank // 2
    return pl.pallas_call(
        functools.partial(assemble_kernel, block_count // 2),
        out_shape=jax.ShapeDtypeStruct(
            (LEVELS, window_cells, block_count * block_cells), jnp.float32
        ),
        in_specs=[
            pl.BlockSpec(memory_space=pltpu.SMEM),
            pl.BlockSpec(memory_space=pltpu.SMEM),
        ]
        + [pl.BlockSpec(memory_space=pltpu.VMEM)] * LEVELS,
        out_specs=pl.BlockSpec(memory_space=pltpu.VMEM),
    )(source_ids.reshape(-1), (slot_rank % 2).reshape(-1), *reply_tables)


def solution(mesh):
    in_specs = (
        P(None, "rows", "cols", None),
        P(None, "rows", "cols", None),
        P(None, ("rows", "cols"), None),
        P(None, ("rows", "cols")),
    )
    out_specs = P(None, None, ("rows", "cols"))
    return jax.shard_map(body, mesh=mesh, in_specs=in_specs, out_specs=out_specs, check_vma=False)
```

profile of v0, /device:TPU:0, one launch (start us, length us, event | category | flops | bytes accessed | tf_op | source)
XLA Modules:
  0.0 340.0 jit_solution(8715704228595878908)
XLA Ops:
  6.5 5.2 %reshape.236 = f32[2,16,2,32,2,256]{5,4,3,2,1,0:T(2,128)} reshape(bf16[2,32,64,256]{3,2,1,0:T(8,128)(2,1)} %param.5) | data formatting | bytes 6291456 | tf_op jit(solution)/shard_map/reshape | solution.py:30
  11.8 5.5 %reduce_sum.42 = f32[2,16,32,256]{3,2,1,0:T(8,128)S(1)} reduce(f32[2,16,2,32,2,256]{5,4,3,2,1,0:T(2,128)} %reshape.236, f32[]{:T(128)} %constant.107.clone.1), dimensions={2,4}, to_apply=%region_4.5 | reduce | flops 786432 | bytes 5242884 | tf_op jit(solution)/shard_map/reduce_sum | solution.py:33
  21.9 5.2 %all-to-all-start = ((s32[8,2,16]{2,1,0:T(2,128)}), s32[8,2,16]{2,1,0:T(2,128)S(1)}, u32[]{:S(2)}, u32[]{:S(2)}) async-start(s32[8,2,16]{2,1,0:T(2,128)} %copy.10), calls=%async_computation | async-start | bytes 16384 | tf_op jit(solution)/shard_map/all_to_all | solution.py:153
  29.3 5.9 %shard_map.47 = bf16[128,64,256]{2,1,0:T(8,128)(2,1)} custom-call(s32[128]{0:T(128)} %reshape_squeeze.15.block_ref, bf16[64,64,256]{2,1,0:T(8,128)(2,1)} %bitcast.36), custom_call_target="tpu_custom_call" | custom-call | tf_op jit(solution)/shard_map/pallas_call | solution.py:163
  35.2 4.6 %all-to-all-start.2 = ((bf16[8,16,64,256]{3,2,1,0:T(8,128)(2,1)}), bf16[8,16,64,256]{3,2,1,0:T(8,128)(2,1)}, u32[]{:S(2)}, u32[]{:S(2)}) async-start(bf16[8,16,64,256]{3,2,1,0:T(8,128)(2,1)} %bitcast.39), calls=%async_computation.2 | async-start | bytes 8388608 | tf_op jit(solution)/shard_map/all_to_all | solution.py:173
  40.4 5.8 %shard_map.46 = bf16[128,64,256]{2,1,0:T(8,128)(2,1)} custom-call(s32[128]{0:T(128)} %reshape_squeeze.13.block_ref, bf16[64,64,256]{2,1,0:T(8,128)(2,1)} %bitcast.37), custom_call_target="tpu_custom_call" | custom-call | tf_op jit(solution)/shard_map/pallas_call | solution.py:163
  46.3 42.6 %all-to-all-done.2 = bf16[8,16,64,256]{3,2,1,0:T(8,128)(2,1)} async-done(((bf16[8,16,64,256]{3,2,1,0:T(8,128)(2,1)}), bf16[8,16,64,256]{3,2,1,0:T(8,128)(2,1)}, u32[]{:S(2)}, u32[]{:S(2)}) %all-to-all-start.2) | async-done | bytes 4194336 | tf_op jit(solution)/shard_map/all_to_all | solution.py:173
  88.9 4.6 %all-to-all-start.1 = ((bf16[8,16,64,256]{3,2,1,0:T(8,128)(2,1)}), bf16[8,16,64,256]{3,2,1,0:T(8,128)(2,1)}, u32[]{:S(2)}, u32[]{:S(2)}) async-start(bf16[8,16,64,256]{3,2,1,0:T(8,128)(2,1)} %bitcast.38), calls=%async_computation.1 | async-start | bytes 8388608 | tf_op jit(solution)/shard_map/all_to_all | solution.py:173
  94.8 2.3 collective-permute-start
  99.0 3.0 collective-permute-done.1
  102.0 2.9 fusion.11
  104.9 3.5 %bitcast_convert_fusion.1.map_ref = f32[48,136,256]{2,1,0:T(8,128)} fusion(bf16[2,24,136,256]{3,2,1,0:T(8,128)(2,1)S(1)} %fusion.11), kind=kLoop, calls=%fused_computation.17 | loop fusion | flops 1671168 | bytes 10027008 | tf_op jit(solution)/shard_map/reshape | solution.py:185
  108.5 11.9 %shard_map.48 = f32[5184,128]{1,0:T(8,128)} custom-call(s32[128]{0:T(128)} %reshape_squeeze.14.label_ref, bf16[128,64,256]{2,1,0:T(8,128)(2,1)} %bitcast.12.query_ref, f32[48,136,256]{2,1,0:T(8,128)} %bitcast_convert_fusion.1.map_ref), custom_call_target="tpu_custom_call" | custom-call | tf_op jit(solution)/shard_map/pallas_call | solution.py:187
  120.4 22.2 %all-to-all-done.1 = bf16[8,16,64,256]{3,2,1,0:T(8,128)(2,1)} async-done(((bf16[8,16,64,256]{3,2,1,0:T(8,128)(2,1)}), bf16[8,16,64,256]{3,2,1,0:T(8,128)(2,1)}, u32[]{:S(2)}, u32[]{:S(2)}) %all-to-all-start.1) | async-done | bytes 4194336 | tf_op jit(solution)/shard_map/all_to_all | solution.py:173
  142.5 63.9 %all_to_all.25 = f32[8,648,128]{2,1,0:T(8,128)} all-to-all(f32[8,648,128]{2,1,0:T(8,128)} %bitcast.43), channel_id=1, replica_groups=mesh['rows'=8,'cols'=4] {'rows'}, dimensions={0} | all-to-all | bytes 5308416 | tf_op jit(solution)/shard_map/all_to_all | solution.py:208
  206.4 10.4 %all-gather.3.cloned.1.call-done = bf16[2,32,256,256]{3,2,1,0:T(8,128)(2,1)} async-done(((bf16[2,32,64,256]{3,2,1,0:T(8,128)(2,1)}), bf16[2,32,256,256]{3,2,1,0:T(8,128)(2,1)}) %all-gather.3.cloned.1.call-update) | async-done | bytes 8388624 | tf_op jit(solution)/shard_map/all_gather | solution.py:180
  222.6 3.5 %collective-permute-done.3 = bf16[2,4,256,256]{3,2,1,0:T(8,128)(2,1)} collective-permute-done((bf16[2,4,256,256]{3,2,1,0:T(8,128)(2,1)S(1)}, bf16[2,4,256,256]{3,2,1,0:T(8,128)(2,1)}, u32[]{:S(2)}, u32[]{:S(2)}) %collective-permute-start.3) | collective-permute-done | bytes 1048608 | tf_op jit(solution)/shard_map/ppermute | solution.py:23
  226.2 11.0 %fusion.5 = bf16[2,40,264,256]{3,2,1,0:T(8,128)(2,1)S(1)} fusion(bf16[2,4,256,256]{3,2,1,0:T(8,128)(2,1)} %collective-permute-done.3, bf16[2,32,256,256]{3,2,1,0:T(8,128)(2,1)} %all-gather.3.cloned.1.call-done, bf16[2,4,256,256]{3,2,1,0:T(8,128)(2,1)S(1)} %collective-permute-done.2), kind=kLoop, calls=%fused_computation.7 | loop fusion | flops 64880640 | bytes 21299200 | tf_op jit(solution)/shard_map/concatenate | solution.py:24
  237.1 7.5 %bitcast_convert_fusion.map_ref = f32[80,264,256]{2,1,0:T(8,128)} fusion(bf16[2,40,264,256]{3,2,1,0:T(8,128)(2,1)S(1)} %fusion.5), kind=kLoop, calls=%fused_computation.8 | loop fusion | flops 5406720 | bytes 32440320 | tf_op jit(solution)/shard_map/reshape | solution.py:185
  244.7 16.1 %shard_map.49 = f32[5184,128]{1,0:T(8,128)} custom-call(s32[128]{0:T(128)} %reshape_squeeze.12.label_ref, bf16[128,64,256]{2,1,0:T(8,128)(2,1)} %bitcast.9.query_ref, f32[80,264,256]{2,1,0:T(8,128)} %bitcast_convert_fusion.map_ref), custom_call_target="tpu_custom_call" | custom-call | tf_op jit(solution)/shard_map/pallas_call | solution.py:187
  260.8 22.8 %all-to-all-start.4 = ((f32[8,648,128]{2,1,0:T(8,128)}), f32[8,648,128]{2,1,0:T(8,128)S(1)}, u32[]{:S(2)}, u32[]{:S(2)}) async-start(f32[8,648,128]{2,1,0:T(8,128)} %bitcast.40), calls=%async_computation.4 | async-start | bytes 5308416 | tf_op jit(solution)/shard_map/all_to_all | solution.py:208
  284.4 31.8 %all-to-all-done.4 = f32[8,648,128]{2,1,0:T(8,128)S(1)} async-done(((f32[8,648,128]{2,1,0:T(8,128)}), f32[8,648,128]{2,1,0:T(8,128)S(1)}, u32[]{:S(2)}, u32[]{:S(2)}) %all-to-all-start.4) | async-done | bytes 2654240 | tf_op jit(solution)/shard_map/all_to_all | solution.py:208
  317.7 10.1 %shard_map.50 = f32[2,81,4096]{2,1,0:T(8,128)} custom-call(s32[128]{0:T(128)} %get-tuple-element.22.source_ref, s32[128]{0:T(128)} %get-tuple-element.21.half_ref, f32[5184,128]{1,0:T(8,128)} %bitcast.42, f32[5184,128]{1,0:T(8,128)} %bitcast.41), custom_call_target="tpu_custom_call" | custom-call | tf_op jit(solution)/shard_map/pallas_call | solution.py:218
  327.8 5.4 %copy.12 = f32[2,81,4096]{2,0,1:T(2,128)} copy(f32[2,81,4096]{2,1,0:T(8,128)} %shard_map.50) | data formatting | bytes 5308416 | tf_op jit(solution)/shard_map/pallas_call | solution.py:218
  (43 shorter events, 18.8 us)
Async XLA Ops:
  6.5 13.0 %copy-start.2 = (s32[2,64,1]{1,2,0:T(1,128)S(1)}, s32[2,64,1]{1,2,0:T(1,128)}, u32[]{:S(2)}) copy-start(s32[2,64,1]{1,2,0:T(1,128)} %param.6) | copy-start | bytes 1540
  6.5 13.9 %copy-start.3 = (s32[2,64]{1,0:T(2,128)S(1)}, s32[2,64]{1,0:T(2,128)}, u32[]{:S(2)}) copy-start(s32[2,64]{1,0:T(2,128)} %param.7) | copy-start | bytes 1540
  6.5 21.2 %copy-start.1 = (bf16[2,32,64,256]{3,2,1,0:T(8,128)(2,1)S(1)}, bf16[2,32,64,256]{3,2,1,0:T(8,128)(2,1)}, u32[]{:S(2)}) copy-start(bf16[2,32,64,256]{3,2,1,0:T(8,128)(2,1)} %param.4) | copy-start | bytes 6291460
  6.5 86.9 %all-gather.5.cloned.1.call-start = ((), (), s32[]{:S(2)}) async-start(), calls=%async_computation.6 | async-start | bytes 2621440 | tf_op jit(solution)/shard_map/all_gather | solution.py:180
  18.2 198.6 %all-gather.3.cloned.1.call-start = ((), (), s32[]{:S(2)}) async-start(), calls=%async_computation.5 | async-start | bytes 10485760 | tf_op jit(solution)/shard_map/all_gather | solution.py:180
  21.9 13.3 %all-to-all-start = ((s32[8,2,16]{2,1,0:T(2,128)}), s32[8,2,16]{2,1,0:T(2,128)S(1)}, u32[]{:S(2)}, u32[]{:S(2)}) async-start(s32[8,2,16]{2,1,0:T(2,128)} %copy.10), calls=%async_computation | async-start | bytes 16384 | tf_op jit(solution)/shard_map/all_to_all | solution.py:153
  35.2 53.7 %all-to-all-start.2 = ((bf16[8,16,64,256]{3,2,1,0:T(8,128)(2,1)}), bf16[8,16,64,256]{3,2,1,0:T(8,128)(2,1)}, u32[]{:S(2)}, u32[]{:S(2)}) async-start(bf16[8,16,64,256]{3,2,1,0:T(8,128)(2,1)} %bitcast.39), calls=%async_computation.2 | async-start | bytes 8388608 | tf_op jit(solution)/shard_map/all_to_all | solution.py:173
  88.9 53.7 %all-to-all-start.1 = ((bf16[8,16,64,256]{3,2,1,0:T(8,128)(2,1)}), bf16[8,16,64,256]{3,2,1,0:T(8,128)(2,1)}, u32[]{:S(2)}, u32[]{:S(2)}) async-start(bf16[8,16,64,256]{3,2,1,0:T(8,128)(2,1)} %bitcast.38), calls=%async_computation.1 | async-start | bytes 8388608 | tf_op jit(solution)/shard_map/all_to_all | solution.py:173
  94.8 4.2 %collective-permute-start = (bf16[2,4,128,256]{3,2,1,0:T(8,128)(2,1)S(1)}, bf16[2,4,128,256]{3,2,1,0:T(8,128)(2,1)S(1)}, u32[]{:S(2)}, u32[]{:S(2)}) collective-permute-start(bf16[2,4,128,256]{3,2,1,0:T(8,128)(2,1)S(1)} %get-tuple-element.13), channel_id=1, source_target_pairs={{0,4},{4,8},{8,12},{12,16},{16,20},{20,24},{24,28},{1,5},{5,9},{9,... | collective-permute-start | bytes 1572872 | tf_op jit(solution)/shard_map/ppermute | solution.py:20
  97.1 4.9 %collective-permute-start.1 = (bf16[2,4,128,256]{3,2,1,0:T(8,128)(2,1)S(1)}, bf16[2,4,128,256]{3,2,1,0:T(8,128)(2,1)S(1)}, u32[]{:S(2)}, u32[]{:S(2)}) collective-permute-start(bf16[2,4,128,256]{3,2,1,0:T(8,128)(2,1)S(1)} %get-tuple-element.14), channel_id=1, source_target_pairs={{4,0},{8,4},{12,8},{16,12},{20,16},{24,20},{28,24},{5,1},{9,5},{13... | collective-permute-start | bytes 1572872 | tf_op jit(solution)/shard_map/ppermute | solution.py:23
  218.5 4.2 %collective-permute-start.2 = (bf16[2,4,256,256]{3,2,1,0:T(8,128)(2,1)S(1)}, bf16[2,4,256,256]{3,2,1,0:T(8,128)(2,1)S(1)}, u32[]{:S(2)}, u32[]{:S(2)}) collective-permute-start(bf16[2,4,256,256]{3,2,1,0:T(8,128)(2,1)S(1)} %get-tuple-element.11), channel_id=1, source_target_pairs={{0,4},{4,8},{8,12},{12,16},{16,20},{20,24},{24,28},{1,5},{5,9},{9,... | collective-permute-start | bytes 3145736 | tf_op jit(solution)/shard_map/ppermute | solution.py:20
  220.4 5.7 %collective-permute-start.3 = (bf16[2,4,256,256]{3,2,1,0:T(8,128)(2,1)S(1)}, bf16[2,4,256,256]{3,2,1,0:T(8,128)(2,1)}, u32[]{:S(2)}, u32[]{:S(2)}) collective-permute-start(bf16[2,4,256,256]{3,2,1,0:T(8,128)(2,1)S(1)} %get-tuple-element.12), channel_id=1, source_target_pairs={{4,0},{8,4},{12,8},{16,12},{20,16},{24,20},{28,24},{5,1},{9,5},{13... | collective-permute-start | bytes 3145736 | tf_op jit(solution)/shard_map/ppermute | solution.py:23
  260.8 55.4 %all-to-all-start.4 = ((f32[8,648,128]{2,1,0:T(8,128)}), f32[8,648,128]{2,1,0:T(8,128)S(1)}, u32[]{:S(2)}, u32[]{:S(2)}) async-start(f32[8,648,128]{2,1,0:T(8,128)} %bitcast.40), calls=%async_computation.4 | async-start | bytes 5308416 | tf_op jit(solution)/shard_map/all_to_all | solution.py:208
  316.2 1.5 copy-start
Sparse Core Ops, SparseCore 0:
  18.3 48.3 all-gather.4
  68.3 148.4 all-gather.2
where the time goes:
time: 341 us; the launch traced here: 340 us
  waiting for transfers between devices  114 us (33%)
  blocking collectives  63.9 us (19%)
  Pallas kernels  49.8 us (15%)
  starting transfers between devices  44.2 us (13%)
  other arithmetic  33.6 us (10%)
  local copies, waits for them, and re-layouts  20.6 us (6%)
  between operations  13.6 us (4%)
    all_to_all x2, waiting for transfers between devices, body(): lax.all_to_all(queries_sent.reshape((row_count,) + slot_block), 'rows', s...  64.8 us
    all_to_all x1, blocking collectives, body(): lax.all_to_all(replies.reshape(row_count, pair_slots * window_cells, 2 *...  63.9 us
    all_to_all x1, waiting for transfers between devices, body(): lax.all_to_all(replies.reshape(row_count, pair_slots * window_cells, 2 *...  31.8 us
    pallas_call x2, Pallas kernels, body(): pl.pallas_call(functools.partial(correlate_kernel, plan, channels ** (-0....  28.1 us
    all_to_all x1, starting transfers between devices, body(): lax.all_to_all(replies.reshape(row_count, pair_slots * window_cells, 2 *...  22.8 us
    concatenate x2, other arithmetic, padded_2(): block = jnp.concatenate([low, block, high], axis=dim)  13.9 us
    pallas_call x2, Pallas kernels, body(): pl.pallas_call(functools.partial(dispatch_kernel, row_slots), out_shape=j...  11.7 us
    reshape x2, other arithmetic, body(): level_map = padded.reshape((-1,) + padded.shape[2:])  11.1 us
  transfers between devices with their start and end apart: 10, of which 7 were waited for; matrix products, arithmetic and copies ran while one was open for 5% of the time, Pallas kernels for 7%

commit v1 on v0

--- a/solution.py
+++ b/solution.py
@@ -229,6 +229,558 @@
     )(source_ids.reshape(-1), (slot_rank % 2).reshape(-1), *reply_tables)
 
 
+MESH = pl.DeviceIdType.MESH
+
+
+def flipped(index, bit):
+    return index + bit - 2 * bit * (index // bit % 2)
+
+
+def chosen(index, values):
+    result = jnp.int32(values[0])
+    for at in range(1, len(values)):
+        result = jnp.where(index == at, values[at], result)
+    return result
+
+
+def plane_plan(count):
+    order, done = [], []
+    for here in range(count):
+        need = [
+            max(abs(near - here) for near in range(max(b - 1, 0), min(b + 2, count)))
+            for b in range(count)
+        ]
+        ranked = sorted(range(count), key=lambda b: (need[b], abs(b - here)))
+        order.append(ranked)
+        done.append([sum(n <= step for n in need) for step in range(count)])
+    return order, done
+
+
+def lookup_kernel(
+    plan,
+    f2_hbm,
+    q_hbm,
+    tab_hbm,
+    rep_out,
+    f2x,
+    f1a,
+    tabv,
+    tabs,
+    map0,
+    map1,
+    p1x,
+    tmp,
+    reps,
+    loc_sem,
+    zs_sem,
+    zr_sem,
+    hs_sem,
+    hr_sem,
+    fs_sem,
+    fr_sem,
+    ts_sem,
+    tr_sem,
+    tl_sem,
+    rs_sem,
+    rr_sem,
+):
+    row_count, plane_count, slots, scale = plan
+    frame_count, band_rows, band_cols, channels = f2_hbm.shape
+    block_count, block_cells, _ = q_hbm.shape
+    side = 2 * RADIUS
+    span = 4 * RADIUS
+    wside = 2 * RADIUS + 1
+    subs = band_rows // side
+    across = band_cols // side
+    half_blocks = block_count // 2
+    r = lax.axis_index("rows")
+    c = lax.axis_index("cols")
+    last_r, last_c = row_count - 1, plane_count - 1
+    order, done = plane_plan(plane_count)
+    sub_order = [0, subs - 1] + list(range(1, subs - 1))
+
+    barrier = pltpu.get_barrier_semaphore()
+    for k in range(1, row_count):
+        pl.semaphore_signal(
+            barrier, inc=1, device_id=((r + k) % row_count, c), device_id_type=MESH
+        )
+
+    @pl.when(c > 0)
+    def _():
+        pl.semaphore_signal(barrier, inc=1, device_id=(r, c - 1), device_id_type=MESH)
+
+    @pl.when(c < last_c)
+    def _():
+        pl.semaphore_signal(barrier, inc=1, device_id=(r, c + 1), device_id_type=MESH)
+
+    has_left = jnp.where(c > 0, 1, 0)
+    has_right = jnp.where(c < last_c, 1, 0)
+    pl.semaphore_wait(barrier, row_count - 1 + has_left + has_right)
+
+    def center(b, sub):
+        return f2x.at[b, :, pl.ds(side + sub * side, side)]
+
+    def z_copy(b, sub, way, own=False):
+        source = f2_hbm.at[:, pl.ds(sub * side, side)] if own else center(b, sub)
+        return pltpu.make_async_remote_copy(
+            src_ref=source,
+            dst_ref=center(b, sub),
+            send_sem=zs_sem.at[way, b, sub],
+            recv_sem=zr_sem.at[b, sub],
+            device_id=(r, c - 1 if way == 0 else c + 1),
+            device_id_type=MESH,
+        )
+
+    def halo_copy(b, way, own=False):
+        sub = 0 if way == 0 else subs - 1
+        at = band_rows + side if way == 0 else 0
+        source = f2_hbm.at[:, pl.ds(sub * side, side)] if own else center(b, sub)
+        return pltpu.make_async_remote_copy(
+            src_ref=source,
+            dst_ref=f2x.at[b, :, pl.ds(at, side)],
+            send_sem=hs_sem.at[way, b],
+            recv_sem=hr_sem.at[way, b],
+            device_id=(r - 1 if way == 0 else r + 1, c),
+            device_id_type=MESH,
+        )
+
+    def send_halo(b, sub, own=False):
+        if sub == 0:
+
+            @pl.when(r > 0)
+            def _():
+                halo_copy(b, 0, own).start()
+
+        if sub == subs - 1:
+
+            @pl.when(r < last_r)
+            def _():
+                halo_copy(b, 1, own).start()
+
+    def f1_copy(index, row, half, bit, own=False):
+        part = pl.ds(half * half_blocks, half_blocks)
+        source = q_hbm.at[part] if own else f1a.at[row, part]
+        return pltpu.make_async_remote_copy(
+            src_ref=source,
+            dst_ref=f1a.at[row, part],
+            send_sem=fs_sem.at[index],
+            recv_sem=fr_sem.at[row, half],
+            device_id=(flipped(r, bit), c),
+            device_id_type=MESH,
+        )
+
+    def tab_copy(k):
+        return pltpu.make_async_remote_copy(
+            src_ref=tab_hbm.at[(r + k) % row_count],
+            dst_ref=tabv.at[r],
+            send_sem=ts_sem.at[k],
+            recv_sem=tr_sem.at[k],
+            device_id=((r + k) % row_count, c),
+            device_id_type=MESH,
+        )
+
+    def rep_copy(b, k):
+        s = (r + k) % row_count
+        return pltpu.make_async_remote_copy(
+            src_ref=reps.at[b, s],
+            dst_ref=rep_out.at[:, r, b],
+            send_sem=rs_sem.at[b, k],
+            recv_sem=rr_sem.at[b, k],
+            device_id=(s, c),
+            device_id_type=MESH,
+        )
+
+    def rep_local(b):
+        return pltpu.make_async_copy(reps.at[b, r], rep_out.at[:, r, b], rs_sem.at[b, 0])
+
+    x_row, y_row, d_row = flipped(r, 2), flipped(r, 4), flipped(flipped(r, 2), 4)
+    f1_first = [(0, r, 0, 2), (1, r, 0, 4), (2, r, 1, 2), (3, r, 1, 4), (4, r, 0, 1), (5, r, 1, 1)]
+    f1_second = [
+        (6, x_row, 0, 4),
+        (7, y_row, 1, 2),
+        (8, x_row, 0, 1),
+        (9, x_row, 1, 1),
+        (10, y_row, 0, 1),
+        (11, y_row, 1, 1),
+    ]
+    f1_third = [(12, d_row, 0, 1), (13, d_row, 1, 1)]
+
+    loc_f2 = pltpu.make_async_copy(f2_hbm, f2x.at[c, :, pl.ds(side, band_rows)], loc_sem.at[0])
+    loc_q = pltpu.make_async_copy(q_hbm, f1a.at[r], loc_sem.at[1])
+    loc_tab = pltpu.make_async_copy(tab_hbm.at[r], tabv.at[r], loc_sem.at[2])
+    loc_f2.start()
+    loc_q.start()
+    loc_tab.start()
+    for sub in sub_order:
+
+        @pl.when(c > 0)
+        def _():
+            z_copy(c, sub, 0, True).start()
+
+        @pl.when(c < last_c)
+        def _():
+            z_copy(c, sub, 1, True).start()
+
+    for item in f1_first:
+        f1_copy(*item, own=True).start()
+    for k in range(1, row_count):
+        tab_copy(k).start()
+    for sub in (0, subs - 1):
+        send_halo(c, sub, True)
+
+    @pl.when(r == 0)
+    def _():
+        f2x[:, :, 0:side] = jnp.zeros((plane_count, frame_count, side) + f2x.shape[3:], f2x.dtype)
+
+    @pl.when(r == last_r)
+    def _():
+        f2x[:, :, band_rows + side :] = jnp.zeros(
+            (plane_count, frame_count, side) + f2x.shape[3:], f2x.dtype
+        )
+
+    def each_side(step, act):
+        @pl.when(c + step <= last_c)
+        def _():
+            act(c + step, 0)
+
+        if step > 0:
+
+            @pl.when(c - step >= 0)
+            def _():
+                act(c - step, 1)
+
+    def take(step, sub):
+        def act(b, way):
+            z_copy(b, sub, way).wait_recv()
+
+            @pl.when(c > 0 if way == 0 else c < last_c)
+            def _():
+                z_copy(b, sub, way).start()
+
+            send_halo(b, sub)
+
+        each_side(step, act)
+
+    def pool(b, way):
+        @pl.when(r > 0)
+        def _():
+            halo_copy(b, 1).wait_recv()
+
+        @pl.when(r < last_r)
+        def _():
+            halo_copy(b, 0).wait_recv()
+
+        rows = p1x.shape[2]
+
+        def pool_row(t, carry):
+            f, i = t // rows, t % rows
+            pair = f2x[b, f, pl.ds(2 * i, 2)].astype(jnp.float32)
+            both = pair[0] + pair[1]
+            for lane in range(channels // 128):
+                tmp[lane] = both[:, lane * 128 : (lane + 1) * 128]
+            for lane in range(channels // 128):
+                even = tmp[lane, pl.ds(0, band_cols // 2, stride=2), :]
+                odd = tmp[lane, pl.ds(1, band_cols // 2, stride=2), :]
+                p1x[b, f, i, :, lane * 128 : (lane + 1) * 128] = (even + odd) * 0.25
+            return carry
+
+        lax.fori_loop(0, frame_count * rows, pool_row, 0)
+
+    lane_id = lax.broadcasted_iota(jnp.int32, (1, 1, 2 * block_cells), 2)
+    query_row = lane_id % block_cells // side
+    query_col = lane_id[0] % side
+    is_first = lane_id[0] < block_cells
+
+    def build(b, level):
+        into = (map0, map1)[level]
+        width = band_cols >> level
+        rows = into.shape[0] // frame_count
+        left_b, right_b = jnp.maximum(b - 1, 0), jnp.minimum(b + 1, last_c)
+
+        def build_row(t, carry):
+            f, y = t // rows, t % rows
+            if level == 0:
+                at = y + RADIUS
+                left = f2x[left_b, f, at, width - 2 * side :, :].astype(jnp.float32)[side:]
+                middle = f2x[b, f, at].astype(jnp.float32)
+                right = f2x[right_b, f, at, : 2 * side, :].astype(jnp.float32)[:side]
+            else:
+                left = p1x[left_b, f, y, width - side :, :]
+                middle = p1x[b, f, y]
+                right = p1x[right_b, f, y, :side, :]
+            left = jnp.where(b > 0, left, 0.0)
+            right = jnp.where(b < last_c, right, 0.0)
+            whole = jnp.concatenate([left, middle, right], axis=0)
+            whole = pltpu.roll(whole, whole.shape[0] - RADIUS, 0)
+            into[t] = whole[: width + side].reshape(into.shape[1:])
+            return carry
+
+        lax.fori_loop(0, into.shape[0], build_row, 0)
+
+    def score_pair(b, s, level, pair):
+        from_map = (map0, map1)[level]
+        windows, queries = [], []
+        for half in range(2):
+            at = (b * LEVELS + level) * slots + 2 * pair + half
+            k, row = tabs[s, 0, at], tabs[s, 1, at]
+            cells = from_map[pl.ds(row, span), pl.ds(tabs[s, 2, at], 2)]
+            windows.append(cells.reshape(span * span, channels).astype(jnp.bfloat16))
+            queries.append(f1a[s, k])
+        queries = jnp.concatenate(queries, axis=0)
+        first, second = [
+            lax.dot_general(
+                window, queries, (((1,), (1,)), ((), ())), preferred_element_type=jnp.float32
+            )
+            for window in windows
+        ]
+        scores = jnp.where(is_first, first, second).reshape(span, span, 2 * block_cells)
+        for bit in (1, 2, 4):
+            scores = jnp.where((query_row & bit) != 0, scores[bit:], scores[:-bit])
+        flat = scores.reshape(wside * span, 2 * block_cells)
+        for bit in (1, 2, 4):
+            moved = pltpu.roll(flat, flat.shape[0] - bit, 0)
+            flat = jnp.where((query_col & bit) != 0, moved, flat)
+        flat = flat * scale
+        for a in range(wside):
+            reps[b, s, level, pair, a * wside : (a + 1) * wside, :] = flat[
+                a * span : a * span + wside
+            ]
+
+    code = chosen(c, [sum(b * plane_count**i for i, b in enumerate(row)) for row in order])
+
+    def process(i, carry):
+        power = chosen(i, [plane_count**n for n in range(plane_count)])
+        b = code // power % plane_count
+        for level in range(LEVELS):
+            build(b, level)
+
+        def source(k, inner):
+            s = (r + k) % row_count
+            for level in range(LEVELS):
+                for pair in range(slots // 2):
+                    score_pair(b, s, level, pair)
+
+            @pl.when(k == 0)
+            def _():
+                rep_local(b).start()
+
+            @pl.when(k > 0)
+            def _():
+                rep_copy(b, k).start()
+
+            return inner
+
+        lax.fori_loop(0, row_count, source, 0)
+        return carry
+
+    def process_ready(step):
+        low = chosen(c, [row[step - 1] for row in done])
+        high = chosen(c, [row[step] for row in done])
+        lax.fori_loop(low, high, process, 0)
+
+    for sub in sub_order:
+        take(1, sub)
+    for item in f1_second:
+        index, row, half, bit = item
+        if index in (6, 7, 9, 10):
+            f1_copy(*item).wait_recv()
+        f1_copy(*item).start()
+    if plane_count > 2:
+        for sub in sub_order[:2]:
+            take(2, sub)
+    for item in f1_third:
+        f1_copy(*item).wait_recv()
+        f1_copy(*item).start()
+    for bits in ((1,), (1, 2), (1, 4), (1, 2, 4)):
+        row = r
+        for bit in bits:
+            row = flipped(row, bit)
+        for half in range(2):
+            f1_copy(0, row, half, 1).wait_recv()
+    for k in range(1, row_count):
+        tab_copy(k).wait_recv()
+    loc_tab.wait()
+    loc_q.wait()
+    loc_f2.wait()
+    tab_smem = pltpu.make_async_copy(tabv, tabs, tl_sem)
+    tab_smem.start()
+    tab_smem.wait()
+    each_side(0, pool)
+    each_side(1, pool)
+    process_ready(1)
+    for step in range(2, plane_count):
+        for sub in sub_order[2:] if step == 2 else sub_order:
+            take(step, sub)
+        each_side(step, pool)
+        process_ready(step)
+
+    for step in range(plane_count):
+        for sub in range(subs):
+
+            def sent(b, way):
+                @pl.when(c > 0 if way == 0 else c < last_c)
+                def _():
+                    z_copy(b, sub, way).wait_send()
+
+            each_side(step, sent)
+            if step == 0:
+
+                @pl.when(c < last_c)
+                def _():
+                    z_copy(c, sub, 1).wait_send()
+
+    def plane_end(b, carry):
+        @pl.when(r > 0)
+        def _():
+            halo_copy(b, 0).wait_send()
+
+        @pl.when(r < last_r)
+        def _():
+            halo_copy(b, 1).wait_send()
+
+        rep_local(b).wait()
+
+        def peer_end(k, inner):
+            rep_copy(b, k).wait_send()
+            rep_copy(b, k).wait_recv()
+            return inner
+
+        lax.fori_loop(1, row_count, peer_end, 0)
+        return carry
+
+    lax.fori_loop(0, plane_count, plane_end, 0)
+    for item in f1_first + f1_second + f1_third:
+        f1_copy(*item).wait_send()
+    for k in range(1, row_count):
+        tab_copy(k).wait_send()
+
+
+def join_kernel(pair_count, source_ref, half_ref, reply_ref, out_ref):
+    level = pl.program_id(0)
+    window_cells, lanes = out_ref.shape[1], reply_ref.shape[-1]
+    is_first = lax.broadcasted_iota(jnp.int32, (window_cells, lanes), 1) < lanes // 2
+
+    def step(m, carry):
+        at = 2 * (level * pair_count + m)
+        picked = []
+        for side in range(2):
+            rows = reply_ref[0, source_ref[at + side], :window_cells, :]
+            moved = pltpu.roll(rows, lanes // 2, 1)
+            picked.append(jnp.where(half_ref[at + side] == side, rows, moved))
+        spot = pl.ds(pl.multiple_of(m * lanes, lanes), lanes)
+        out_ref[0, :, spot] = jnp.where(is_first, picked[0], picked[1])
+        return carry
+
+    lax.fori_loop(0, pair_count, step, 0)
+
+
+def gathered_body(fmap1, fmap2, target_owner, target_tile):
+    side = 2 * RADIUS
+    window_cells = (2 * RADIUS + 1) ** 2
+    frame_count, band_rows, band_cols, channels = fmap1.shape
+    row_count = lax.axis_size("rows")
+    plane_count = lax.axis_size("cols")
+    device_count = row_count * plane_count
+    subs, across = band_rows // side, band_cols // side
+    per_frame = subs * across
+    block_count = frame_count * per_frame
+    block_cells = side * side
+    slots = max(2, (2 * block_count + device_count - 1) // device_count)
+    queries = fmap1.reshape(frame_count, subs, side, across, side, channels)
+    queries = queries.transpose(0, 1, 3, 2, 4, 5).reshape(block_count, block_cells, channels)
+
+    owner = target_owner[:, :, 0]
+    owner_ids = jnp.arange(device_count, dtype=jnp.int32)
+    hits = (owner[:, :, None] == owner_ids).astype(jnp.int32)
+    rank = jnp.sum(hits * (jnp.cumsum(hits, axis=1) - 1), axis=2)
+    block_ids = jnp.arange(block_count, dtype=jnp.int32)
+    entries = []
+    for level in range(LEVELS):
+        level_across = across >> level
+        tile = target_tile[level] % ((subs >> level) * level_across)
+        map_rows = (band_rows >> level) + side
+        row = block_ids // per_frame * map_rows + tile // level_across * side
+        entries.append(jnp.stack([block_ids, row, tile % level_across]))
+    entries = jnp.stack(entries, axis=1)
+    ranked = (rank[:, :, None] == jnp.arange(slots, dtype=jnp.int32)).astype(jnp.int32)
+    table = jnp.sum(
+        hits[:, :, :, None] * ranked[:, :, None, :] * entries[:, :, :, None, None], axis=2
+    )
+    table = table.reshape(3, LEVELS, row_count, plane_count, slots).transpose(2, 0, 3, 1, 4)
+    used = plane_count * LEVELS * slots
+    table = table.reshape(row_count, 3, used)
+    table = jnp.pad(table, ((0, 0), (0, 5), (0, -used % 128)))
+
+    padded_rows = -(-window_cells // 8) * 8
+    pairs = slots // 2
+    reply_shape = (LEVELS, row_count, plane_count, pairs, padded_rows, 2 * block_cells)
+    ext_rows = band_rows + 2 * side
+    dma = pltpu.SemaphoreType.DMA
+    replies = pl.pallas_call(
+        functools.partial(lookup_kernel, (row_count, plane_count, slots, channels**-0.5)),
+        out_shape=jax.ShapeDtypeStruct(reply_shape, jnp.float32),
+        in_specs=[pl.BlockSpec(memory_space=pl.ANY)] * 3,
+        out_specs=pl.BlockSpec(memory_space=pl.ANY),
+        scratch_shapes=[
+            pltpu.VMEM((plane_count, frame_count, ext_rows, band_cols, channels), jnp.bfloat16),
+            pltpu.VMEM((row_count, block_count, block_cells, channels), jnp.bfloat16),
+            pltpu.VMEM(table.shape, jnp.int32),
+            pltpu.SMEM(table.shape, jnp.int32),
+            pltpu.VMEM((frame_count * (band_rows + side), across + 1, side, channels), jnp.float32),
+            pltpu.VMEM(
+                (frame_count * (band_rows // 2 + side), across // 2 + 1, side, channels),
+                jnp.float32,
+            ),
+            pltpu.VMEM(
+                (plane_count, frame_count, ext_rows // 2, band_cols // 2, channels), jnp.float32
+            ),
+            pltpu.VMEM((channels // 128, band_cols, 128), jnp.float32),
+            pltpu.VMEM(
+                (plane_count, row_count, LEVELS, pairs, padded_rows, 2 * block_cells), jnp.float32
+            ),
+            dma((3,)),
+            dma((2, plane_count, subs)),
+            dma((plane_count, subs)),
+            dma((2, plane_count)),
+            dma((2, plane_count)),
+            dma((14,)),
+            dma((row_count, 2)),
+            dma((row_count,)),
+            dma((row_count,)),
+            dma,
+            dma((plane_count, row_count)),
+            dma((plane_count, row_count)),
+        ],
+        compiler_params=pltpu.CompilerParams(
+            collective_id=0, has_side_effects=True, vmem_limit_bytes=62 * 2**20
+        ),
+    )(fmap2, queries, table)
+    spots = row_count * plane_count * pairs
+    source_ids = owner * pairs + rank // 2
+    return pl.pallas_call(
+        functools.partial(join_kernel, block_count // 2),
+        out_shape=jax.ShapeDtypeStruct(
+            (LEVELS, window_cells, block_count * block_cells), jnp.float32
+        ),
+        grid_spec=pltpu.PrefetchScalarGridSpec(
+            num_scalar_prefetch=2,
+            grid=(LEVELS,),
+            in_specs=[
+                pl.BlockSpec(
+                    (1, spots, padded_rows, 2 * block_cells), lambda l, *_: (l, 0, 0, 0)
+                )
+            ],
+            out_specs=pl.BlockSpec(
+                (1, window_cells, block_count * block_cells), lambda l, *_: (l, 0, 0)
+            ),
+        ),
+    )(
+        source_ids.reshape(-1),
+        (rank % 2).reshape(-1),
+        replies.reshape(LEVELS, spots, padded_rows, 2 * block_cells),
+    )
+
+
 def solution(mesh):
     in_specs = (
         P(None, "rows", "cols", None),
@@ -237,4 +789,7 @@
         P(None, ("rows", "cols")),
     )
     out_specs = P(None, None, ("rows", "cols"))
-    return jax.shard_map(body, mesh=mesh, in_specs=in_specs, out_specs=out_specs, check_vma=False)
+    chosen_body = gathered_body if mesh.shape["rows"] == 8 else body
+    return jax.shard_map(
+        chosen_body, mesh=mesh, in_specs=in_specs, out_specs=out_specs, check_vma=False
+    )

time: 341 us -> 216 us (0.63)
  Pallas kernels: 49.8 us -> 202 us
  waiting for transfers between devices: 114 us -> 0 us
  blocking collectives: 63.9 us -> 0 us
  starting transfers between devices: 44.2 us -> 0 us
  other arithmetic: 33.6 us -> 4.28 us
  between operations: 13.6 us -> 0.07 us
  local copies, waits for them, and re-layouts: 20.6 us -> 9.81 us
    pallas_call x5 -> x2, Pallas kernels: 49.8 us -> 202 us  [the longest x1 192 us: gathered_body(): pl.pallas_call(functools.partial(lookup_kernel, (row_count, plane_count,...]
    all_to_all x4 -> x0, waiting for transfers between devices: 96.6 us -> none  [the longest x2 64.8 us: body(): lax.all_to_all(queries_sent.reshape((row_count,) + slot_block), 'rows', s...]
    all_to_all x1 -> x0, blocking collectives: 63.9 us -> none  [body(): lax.all_to_all(replies.reshape(row_count, pair_slots * window_cells, 2 *...]
    all_to_all x4 -> x0, starting transfers between devices: 37.2 us -> none  [the longest x1 22.8 us: body(): lax.all_to_all(replies.reshape(row_count, pair_slots * window_cells, 2 *...]
    concatenate x2 -> x0, other arithmetic: 13.9 us -> none  [padded_2(): block = jnp.concatenate([low, block, high], axis=dim)]
    reshape x2 -> x0, other arithmetic: 11.1 us -> none  [body(): level_map = padded.reshape((-1,) + padded.shape[2:])]
    all_gather x2 -> x0, waiting for transfers between devices: 10.4 us -> none  [body(): band = lax.all_gather(levels[level], 'cols', axis=2, tiled=True)]
    ppermute x4 -> x0, starting transfers between devices: 7.02 us -> none  [the longest x2 4.26 us: padded_2(): lax.ppermute(lax.slice_in_dim(block, block.shape[dim] - width, None, axis...]
  transfers between devices with their start and end apart: 10 -> 0, of which waited for: 7 -> 0; matrix products, arithmetic and copies ran while one was open for 5% -> 0% of each run, Pallas kernels for 7% -> 0%
where the time goes in v1:
time: 216 us
  Pallas kernels  202 us (94%)
  local copies, waits for them, and re-layouts  9.81 us (5%)
  other arithmetic  4.28 us (2%)
    pallas_call x1, Pallas kernels, gathered_body(): pl.pallas_call(functools.partial(lookup_kernel, (row_count, plane_count,...  192 us
    pallas_call x1, Pallas kernels, gathered_body(): pl.pallas_call(functools.partial(join_kernel, block_count // 2), out_shap...  9.59 us
    pallas_call x1, local copies, waits for them, and re-layouts, gathered_body(): pl.pallas_call(functools.partial(join_kernel, block_count // 2), out_shap...  5.36 us

profile of v1, /device:TPU:0, one launch (start us, length us, event | category | flops | bytes accessed | tf_op | source)
XLA Modules:
  0.0 215.9 jit_solution(584755325858392796)
XLA Ops:
  0.0 0.7 multiply_reduce_fusion.1
  0.7 0.1 mul.81
  0.8 0.8 multiply_add_fusion.1
  1.6 0.8 fusion
  2.4 0.1 copy.14
  2.5 0.1 reduce_window_sum.11
  2.6 0.9 select_reduce_fusion
  3.4 0.1 reduce_sum.21
  3.5 0.5 and_select_fusion.7
  4.1 0.5 multiply_reduce_fusion
  4.6 0.1 reshape.76
  4.7 0.2 copy.16
  4.9 0.1 copy.17
  5.0 0.6 pad.4.tab_hbm
  5.6 3.2 %copy.13 = bf16[2,4,8,8,8,256]{5,4,2,3,1,0:T(8,128)(2,1)} copy(bf16[2,4,8,8,8,256]{5,4,3,2,1,0:T(8,128)(2,1)} %bitcast.16) | data formatting | bytes 4194304 | tf_op jit(solution)/shard_map/reshape | solution.py:689
  8.8 192.1 %shard_map.46 = f32[2,8,4,2,88,128]{5,4,3,2,1,0:T(8,128)} custom-call(bf16[2,32,64,256]{3,2,1,0:T(8,128)(2,1)} %f2_hbm.1, bf16[64,64,256]{2,1,0:T(8,128)(2,1)} %bitcast.15, s32[8,8,128]{2,1,0:T(8,128)} %pad.4.tab_hbm), custom_call_target="tpu_custom_call" | custom-call | tf_op jit(solution)/shard_map/pallas_call | solution.py:719
  201.0 9.6 %shard_map.47 = f32[2,81,4096]{2,1,0:T(8,128)} custom-call(s32[128]{0:T(128)} %get-tuple-element.14.source_ref, s32[128]{0:T(128)} %get-tuple-element.13.half_ref, f32[2,64,88,128]{3,2,1,0:T(8,128)} %bitcast.14), custom_call_target="tpu_custom_call" | custom-call | tf_op jit(solution)/shard_map/pallas_call | solution.py:760
  210.5 5.4 %copy.18 = f32[2,81,4096]{2,0,1:T(2,128)} copy(f32[2,81,4096]{2,1,0:T(8,128)} %shard_map.47) | data formatting | bytes 5308416 | tf_op jit(solution)/shard_map/pallas_call | solution.py:760
  (7 shorter events, 0.1 us)

commit v2 on v1

--- a/solution.py
+++ b/solution.py
@@ -230,30 +230,11 @@
 
 
 MESH = pl.DeviceIdType.MESH
+TOP = 32767.0
 
 
 def flipped(index, bit):
     return index + bit - 2 * bit * (index // bit % 2)
-
-
-def chosen(index, values):
-    result = jnp.int32(values[0])
-    for at in range(1, len(values)):
-        result = jnp.where(index == at, values[at], result)
-    return result
-
-
-def plane_plan(count):
-    order, done = [], []
-    for here in range(count):
-        need = [
-            max(abs(near - here) for near in range(max(b - 1, 0), min(b + 2, count)))
-            for b in range(count)
-        ]
-        ranked = sorted(range(count), key=lambda b: (need[b], abs(b - here)))
-        order.append(ranked)
-        done.append([sum(n <= step for n in need) for step in range(count)])
-    return order, done
 
 
 def lookup_kernel(
@@ -270,6 +251,7 @@
     map1,
     p1x,
     tmp,
+    line,
     reps,
     loc_sem,
     zs_sem,
@@ -290,14 +272,12 @@
     side = 2 * RADIUS
     span = 4 * RADIUS
     wside = 2 * RADIUS + 1
-    subs = band_rows // side
-    across = band_cols // side
+    wide = 2 * side
+    strips = band_cols // wide
     half_blocks = block_count // 2
     r = lax.axis_index("rows")
     c = lax.axis_index("cols")
     last_r, last_c = row_count - 1, plane_count - 1
-    order, done = plane_plan(plane_count)
-    sub_order = [0, subs - 1] + list(range(1, subs - 1))
 
     barrier = pltpu.get_barrier_semaphore()
     for k in range(1, row_count):
@@ -317,45 +297,47 @@
     has_right = jnp.where(c < last_c, 1, 0)
     pl.semaphore_wait(barrier, row_count - 1 + has_left + has_right)
 
-    def center(b, sub):
-        return f2x.at[b, :, pl.ds(side + sub * side, side)]
-
-    def z_copy(b, sub, way, own=False):
-        source = f2_hbm.at[:, pl.ds(sub * side, side)] if own else center(b, sub)
+    def strip(at, way):
+        return at if way == 0 else strips - 1 - at
+
+    def z_copy(b, at, way, own=False):
+        cols = pl.ds(strip(at, way) * wide, wide)
+        here = f2x.at[b, :, pl.ds(side, band_rows), cols]
+        return pltpu.make_async_remote_copy(
+            src_ref=f2_hbm.at[:, :, cols] if own else here,
+            dst_ref=here,
+            send_sem=zs_sem.at[way, b, at],
+            recv_sem=zr_sem.at[b, at],
+            device_id=(r, c - 1 if way == 0 else c + 1),
+            device_id_type=MESH,
+        )
+
+    def halo_copy(b, at, way, up, own=False):
+        cols = pl.ds(strip(at, way) * wide, wide)
+        first = 0 if up else band_rows - side
+        into = band_rows + side if up else 0
+        if own:
+            source = f2_hbm.at[:, pl.ds(first, side), cols]
+        else:
+            source = f2x.at[b, :, pl.ds(first + side, side), cols]
+        lane = 0 if up else 1
         return pltpu.make_async_remote_copy(
             src_ref=source,
-            dst_ref=center(b, sub),
-            send_sem=zs_sem.at[way, b, sub],
-            recv_sem=zr_sem.at[b, sub],
-            device_id=(r, c - 1 if way == 0 else c + 1),
+            dst_ref=f2x.at[b, :, pl.ds(into, side), cols],
+            send_sem=hs_sem.at[lane, b, at],
+            recv_sem=hr_sem.at[lane, b, at],
+            device_id=(r - 1 if up else r + 1, c),
             device_id_type=MESH,
         )
 
-    def halo_copy(b, way, own=False):
-        sub = 0 if way == 0 else subs - 1
-        at = band_rows + side if way == 0 else 0
-        source = f2_hbm.at[:, pl.ds(sub * side, side)] if own else center(b, sub)
-        return pltpu.make_async_remote_copy(
-            src_ref=source,
-            dst_ref=f2x.at[b, :, pl.ds(at, side)],
-            send_sem=hs_sem.at[way, b],
-            recv_sem=hr_sem.at[way, b],
-            device_id=(r - 1 if way == 0 else r + 1, c),
-            device_id_type=MESH,
-        )
-
-    def send_halo(b, sub, own=False):
-        if sub == 0:
-
-            @pl.when(r > 0)
-            def _():
-                halo_copy(b, 0, own).start()
-
-        if sub == subs - 1:
-
-            @pl.when(r < last_r)
-            def _():
-                halo_copy(b, 1, own).start()
+    def send_halo(b, at, way, own=False):
+        @pl.when(r > 0)
+        def _():
+            halo_copy(b, at, way, True, own).start()
+
+        @pl.when(r < last_r)
+        def _():
+            halo_copy(b, at, way, False, own).start()
 
     def f1_copy(index, row, half, bit, own=False):
         part = pl.ds(half * half_blocks, half_blocks)
@@ -411,22 +393,22 @@
     loc_f2.start()
     loc_q.start()
     loc_tab.start()
-    for sub in sub_order:
+    for at in range(strips):
 
         @pl.when(c > 0)
         def _():
-            z_copy(c, sub, 0, True).start()
+            z_copy(c, at, 0, True).start()
 
         @pl.when(c < last_c)
         def _():
-            z_copy(c, sub, 1, True).start()
+            z_copy(c, at, 1, True).start()
 
     for item in f1_first:
         f1_copy(*item, own=True).start()
     for k in range(1, row_count):
         tab_copy(k).start()
-    for sub in (0, subs - 1):
-        send_halo(c, sub, True)
+    for at in range(strips):
+        send_halo(c, at, 0, True)
 
     @pl.when(r == 0)
     def _():
@@ -449,47 +431,59 @@
             def _():
                 act(c - step, 1)
 
-    def take(step, sub):
+    def take(step, at):
         def act(b, way):
-            z_copy(b, sub, way).wait_recv()
+            z_copy(b, at, way).wait_recv()
 
             @pl.when(c > 0 if way == 0 else c < last_c)
             def _():
-                z_copy(b, sub, way).start()
-
-            send_halo(b, sub)
+                z_copy(b, at, way).start()
+
+            send_halo(b, at, way)
 
         each_side(step, act)
 
-    def pool(b, way):
-        @pl.when(r > 0)
-        def _():
-            halo_copy(b, 1).wait_recv()
-
-        @pl.when(r < last_r)
-        def _():
-            halo_copy(b, 0).wait_recv()
-
-        rows = p1x.shape[2]
-
-        def pool_row(t, carry):
-            f, i = t // rows, t % rows
-            pair = f2x[b, f, pl.ds(2 * i, 2)].astype(jnp.float32)
-            both = pair[0] + pair[1]
-            for lane in range(channels // 128):
-                tmp[lane] = both[:, lane * 128 : (lane + 1) * 128]
-            for lane in range(channels // 128):
-                even = tmp[lane, pl.ds(0, band_cols // 2, stride=2), :]
-                odd = tmp[lane, pl.ds(1, band_cols // 2, stride=2), :]
-                p1x[b, f, i, :, lane * 128 : (lane + 1) * 128] = (even + odd) * 0.25
-            return carry
-
-        lax.fori_loop(0, frame_count * rows, pool_row, 0)
+    def pool(step, ats):
+        def act(b, way):
+            for at in ats:
+
+                @pl.when(r > 0)
+                def _():
+                    halo_copy(b, at, way, False).wait_recv()
+
+                @pl.when(r < last_r)
+                def _():
+                    halo_copy(b, at, way, True).wait_recv()
+
+            rows = p1x.shape[2]
+            for at in ats:
+                col = strip(at, way)
+
+                def pool_row(t, carry):
+                    f, i = t // rows, t % rows
+                    pair = f2x[b, f, pl.ds(2 * i, 2), col * wide : (col + 1) * wide]
+                    pair = pair.astype(jnp.float32)
+                    both = pair[0] + pair[1]
+                    for lane in range(channels // 128):
+                        tmp[lane, pl.ds(i * wide, wide), :] = both[:, lane * 128 : (lane + 1) * 128]
+                    for lane in range(channels // 128):
+                        even = tmp[lane, pl.ds(i * wide, side, stride=2), :]
+                        odd = tmp[lane, pl.ds(i * wide + 1, side, stride=2), :]
+                        p1x[
+                            b, f, i, col * side : (col + 1) * side, lane * 128 : (lane + 1) * 128
+                        ] = (even + odd) * 0.25
+                    return carry
+
+                lax.fori_loop(0, frame_count * rows, pool_row, 0, unroll=4)
+
+        each_side(step, act)
 
     lane_id = lax.broadcasted_iota(jnp.int32, (1, 1, 2 * block_cells), 2)
     query_row = lane_id % block_cells // side
     query_col = lane_id[0] % side
     is_first = lane_id[0] < block_cells
+    row_id = lax.broadcasted_iota(jnp.int32, line.shape[1:], 0)
+    line[...] = jnp.zeros(line.shape, line.dtype)
 
     def build(b, level):
         into = (map0, map1)[level]
@@ -542,15 +536,16 @@
             flat = jnp.where((query_col & bit) != 0, moved, flat)
         flat = flat * scale
         for a in range(wside):
-            reps[b, s, level, pair, a * wside : (a + 1) * wside, :] = flat[
-                a * span : a * span + wside
-            ]
-
-    code = chosen(c, [sum(b * plane_count**i for i, b in enumerate(row)) for row in order])
-
-    def process(i, carry):
-        power = chosen(i, [plane_count**n for n in range(plane_count)])
-        b = code // power % plane_count
+            line[pair, a * wside : (a + 1) * wside, :] = flat[a * span : a * span + wside]
+        found = line[pair]
+        top = jnp.max(jnp.abs(found), axis=0, keepdims=True)
+        power = jnp.maximum(jnp.ceil(jnp.log2(top)), -100.0)
+        coded = jnp.floor(found * (TOP * jnp.exp2(-power)) + 0.5)
+        coded = jnp.clip(coded, -TOP, TOP)
+        coded = jnp.where(row_id == wside * wside, power, coded)
+        reps[b, s, level, pair] = coded.astype(jnp.int32).astype(jnp.int16)
+
+    def process(b, way):
         for level in range(LEVELS):
             build(b, level)
 
@@ -571,23 +566,16 @@
             return inner
 
         lax.fori_loop(0, row_count, source, 0)
-        return carry
-
-    def process_ready(step):
-        low = chosen(c, [row[step - 1] for row in done])
-        high = chosen(c, [row[step] for row in done])
-        lax.fori_loop(low, high, process, 0)
-
-    for sub in sub_order:
-        take(1, sub)
+
+    for at in range(strips):
+        take(1, at)
     for item in f1_second:
         index, row, half, bit = item
         if index in (6, 7, 9, 10):
             f1_copy(*item).wait_recv()
         f1_copy(*item).start()
-    if plane_count > 2:
-        for sub in sub_order[:2]:
-            take(2, sub)
+    for at in range(strips - 1):
+        take(2, at)
     for item in f1_third:
         f1_copy(*item).wait_recv()
         f1_copy(*item).start()
@@ -605,39 +593,48 @@
     tab_smem = pltpu.make_async_copy(tabv, tabs, tl_sem)
     tab_smem.start()
     tab_smem.wait()
-    each_side(0, pool)
-    each_side(1, pool)
-    process_ready(1)
-    for step in range(2, plane_count):
-        for sub in sub_order[2:] if step == 2 else sub_order:
-            take(step, sub)
-        each_side(step, pool)
-        process_ready(step)
+    near, rest = [0], list(range(1, strips))
+    pool(0, near + rest)
+    pool(1, near)
+    each_side(0, process)
+    take(2, strips - 1)
+    for step in range(1, plane_count):
+        if step > 2:
+            for at in rest:
+                take(step, at)
+        if step >= 2 and step + 1 < plane_count:
+            take(step + 1, 0)
+        pool(step, rest)
+        if step + 1 < plane_count:
+            pool(step + 1, near)
+        each_side(step, process)
+
+    for at in range(strips):
+
+        @pl.when(c < last_c)
+        def _():
+            z_copy(c, at, 1).wait_send()
 
     for step in range(plane_count):
-        for sub in range(subs):
-
-            def sent(b, way):
+
+        def sent(b, way):
+            for at in range(strips):
+
                 @pl.when(c > 0 if way == 0 else c < last_c)
                 def _():
-                    z_copy(b, sub, way).wait_send()
-
-            each_side(step, sent)
-            if step == 0:
-
-                @pl.when(c < last_c)
+                    z_copy(b, at, way).wait_send()
+
+                @pl.when(r > 0)
                 def _():
-                    z_copy(c, sub, 1).wait_send()
+                    halo_copy(b, at, way, True).wait_send()
+
+                @pl.when(r < last_r)
+                def _():
+                    halo_copy(b, at, way, False).wait_send()
+
+        each_side(step, sent)
 
     def plane_end(b, carry):
-        @pl.when(r > 0)
-        def _():
-            halo_copy(b, 0).wait_send()
-
-        @pl.when(r < last_r)
-        def _():
-            halo_copy(b, 1).wait_send()
-
         rep_local(b).wait()
 
         def peer_end(k, inner):
@@ -655,23 +652,25 @@
         tab_copy(k).wait_send()
 
 
-def join_kernel(pair_count, source_ref, half_ref, reply_ref, out_ref):
+def join_kernel(pair_count, window_cells, source_ref, half_ref, reply_ref, out_ref):
     level = pl.program_id(0)
-    window_cells, lanes = out_ref.shape[1], reply_ref.shape[-1]
-    is_first = lax.broadcasted_iota(jnp.int32, (window_cells, lanes), 1) < lanes // 2
+    padded_rows, lanes = reply_ref.shape[-2:]
+    is_first = lax.broadcasted_iota(jnp.int32, (padded_rows, lanes), 1) < lanes // 2
 
     def step(m, carry):
         at = 2 * (level * pair_count + m)
         picked = []
         for side in range(2):
-            rows = reply_ref[0, source_ref[at + side], :window_cells, :]
+            rows = reply_ref[0, source_ref[at + side]].astype(jnp.int32).astype(jnp.float32)
             moved = pltpu.roll(rows, lanes // 2, 1)
             picked.append(jnp.where(half_ref[at + side] == side, rows, moved))
-        spot = pl.ds(pl.multiple_of(m * lanes, lanes), lanes)
-        out_ref[0, :, spot] = jnp.where(is_first, picked[0], picked[1])
+        both = jnp.where(is_first, picked[0], picked[1])
+        unit = jnp.exp2(both[window_cells : window_cells + 1]) * (1.0 / TOP)
+        spot = pl.ds(m * LEVELS + level, window_cells, stride=pair_count * LEVELS)
+        out_ref[spot, :] = both[:window_cells] * unit
         return carry
 
-    lax.fori_loop(0, pair_count, step, 0)
+    lax.fori_loop(0, pair_count, step, 0, unroll=2)
 
 
 def gathered_body(fmap1, fmap2, target_owner, target_tile):
@@ -690,35 +689,38 @@
     queries = queries.transpose(0, 1, 3, 2, 4, 5).reshape(block_count, block_cells, channels)
 
     owner = target_owner[:, :, 0]
-    owner_ids = jnp.arange(device_count, dtype=jnp.int32)
-    hits = (owner[:, :, None] == owner_ids).astype(jnp.int32)
-    rank = jnp.sum(hits * (jnp.cumsum(hits, axis=1) - 1), axis=2)
     block_ids = jnp.arange(block_count, dtype=jnp.int32)
-    entries = []
+    earlier = block_ids[:, None] > block_ids[None, :]
+    same = owner[:, :, None] == owner[:, None, :]
+    rank = jnp.sum((same & earlier).astype(jnp.int32), axis=2)
+    values, places = [], []
     for level in range(LEVELS):
         level_across = across >> level
         tile = target_tile[level] % ((subs >> level) * level_across)
         map_rows = (band_rows >> level) + side
         row = block_ids // per_frame * map_rows + tile // level_across * side
-        entries.append(jnp.stack([block_ids, row, tile % level_across]))
-    entries = jnp.stack(entries, axis=1)
-    ranked = (rank[:, :, None] == jnp.arange(slots, dtype=jnp.int32)).astype(jnp.int32)
-    table = jnp.sum(
-        hits[:, :, :, None] * ranked[:, :, None, :] * entries[:, :, :, None, None], axis=2
-    )
-    table = table.reshape(3, LEVELS, row_count, plane_count, slots).transpose(2, 0, 3, 1, 4)
-    used = plane_count * LEVELS * slots
-    table = table.reshape(row_count, 3, used)
-    table = jnp.pad(table, ((0, 0), (0, 5), (0, -used % 128)))
-
-    padded_rows = -(-window_cells // 8) * 8
+        values.append(jnp.stack([block_ids, row, tile % level_across]))
+        places.append((owner[level] % plane_count * LEVELS + level) * slots + rank[level])
+    values = jnp.pad(jnp.concatenate(values, axis=1), ((0, 5), (0, 0)))
+    places = jnp.concatenate(places)
+    towards = owner.reshape(-1) // plane_count
+    lanes_used = -(-plane_count * LEVELS * slots // 128) * 128
+    named = towards == jnp.arange(row_count, dtype=jnp.int32)[:, None]
+    left = jnp.where(named[:, None, :], values[None], 0).astype(jnp.float32)
+    right = (places[:, None] == jnp.arange(lanes_used, dtype=jnp.int32)).astype(jnp.float32)
+    table = lax.dot_general(
+        left, right, (((2,), (0,)), ((), ())), precision=lax.Precision.HIGHEST
+    ).astype(jnp.int32)
+
+    padded_rows = -(-(window_cells + 1) // 16) * 16
     pairs = slots // 2
+    strips = across // 2
     reply_shape = (LEVELS, row_count, plane_count, pairs, padded_rows, 2 * block_cells)
     ext_rows = band_rows + 2 * side
     dma = pltpu.SemaphoreType.DMA
     replies = pl.pallas_call(
         functools.partial(lookup_kernel, (row_count, plane_count, slots, channels**-0.5)),
-        out_shape=jax.ShapeDtypeStruct(reply_shape, jnp.float32),
+        out_shape=jax.ShapeDtypeStruct(reply_shape, jnp.int16),
         in_specs=[pl.BlockSpec(memory_space=pl.ANY)] * 3,
         out_specs=pl.BlockSpec(memory_space=pl.ANY),
         scratch_shapes=[
@@ -734,15 +736,16 @@
             pltpu.VMEM(
                 (plane_count, frame_count, ext_rows // 2, band_cols // 2, channels), jnp.float32
             ),
-            pltpu.VMEM((channels // 128, band_cols, 128), jnp.float32),
+            pltpu.VMEM((channels // 128, ext_rows // 2 * 2 * side, 128), jnp.float32),
+            pltpu.VMEM((pairs, padded_rows, 2 * block_cells), jnp.float32),
             pltpu.VMEM(
-                (plane_count, row_count, LEVELS, pairs, padded_rows, 2 * block_cells), jnp.float32
+                (plane_count, row_count, LEVELS, pairs, padded_rows, 2 * block_cells), jnp.int16
             ),
             dma((3,)),
-            dma((2, plane_count, subs)),
-            dma((plane_count, subs)),
-            dma((2, plane_count)),
-            dma((2, plane_count)),
+            dma((2, plane_count, strips)),
+            dma((plane_count, strips)),
+            dma((2, plane_count, strips)),
+            dma((2, plane_count, strips)),
             dma((14,)),
             dma((row_count, 2)),
             dma((row_count,)),
@@ -757,21 +760,19 @@
     )(fmap2, queries, table)
     spots = row_count * plane_count * pairs
     source_ids = owner * pairs + rank // 2
-    return pl.pallas_call(
-        functools.partial(join_kernel, block_count // 2),
+    joined = pl.pallas_call(
+        functools.partial(join_kernel, block_count // 2, window_cells),
         out_shape=jax.ShapeDtypeStruct(
-            (LEVELS, window_cells, block_count * block_cells), jnp.float32
+            (window_cells * block_count // 2 * LEVELS, 2 * block_cells), jnp.float32
         ),
         grid_spec=pltpu.PrefetchScalarGridSpec(
             num_scalar_prefetch=2,
             grid=(LEVELS,),
             in_specs=[
-                pl.BlockSpec(
-                    (1, spots, padded_rows, 2 * block_cells), lambda l, *_: (l, 0, 0, 0)
-                )
+                pl.BlockSpec((1, spots, padded_rows, 2 * block_cells), lambda l, *_: (l, 0, 0, 0))
             ],
             out_specs=pl.BlockSpec(
-                (1, window_cells, block_count * block_cells), lambda l, *_: (l, 0, 0)
+                (window_cells * block_count // 2 * LEVELS, 2 * block_cells), lambda l, *_: (0, 0)
             ),
         ),
     )(
@@ -779,6 +780,8 @@
         (rank % 2).reshape(-1),
         replies.reshape(LEVELS, spots, padded_rows, 2 * block_cells),
     )
+    joined = joined.reshape(window_cells, block_count // 2, LEVELS, 2 * block_cells)
+    return joined.transpose(2, 0, 1, 3).reshape(LEVELS, window_cells, block_count * block_cells)
 
 
 def solution(mesh):

time: 216 us -> 183 us (0.85)
  Pallas kernels: 202 us -> 173 us
  local copies, waits for them, and re-layouts: 9.81 us -> 3.88 us
    pallas_call x1, Pallas kernels: 192 us -> 164 us  [gathered_body(): pl.pallas_call(functools.partial(lookup_kernel, (row_count, plane_count,...]
    pallas_call x1 -> x0, local copies, waits for them, and re-layouts: 5.36 us -> none  [gathered_body(): pl.pallas_call(functools.partial(join_kernel, block_count // 2), out_shap...]
where the time goes in v2:
time: 183 us; the launch traced here: 182 us
  Pallas kernels  173 us (95%)
  other arithmetic  4.53 us (2%)
  local copies, waits for them, and re-layouts  3.88 us (2%)
    pallas_call x1, Pallas kernels, gathered_body(): pl.pallas_call(functools.partial(lookup_kernel, (row_count, plane_count,...  164 us
    pallas_call x1, Pallas kernels, gathered_body(): pl.pallas_call(functools.partial(join_kernel, block_count // 2, window_ce...  9.07 us

profile of v2, /device:TPU:0, one launch (start us, length us, event | category | flops | bytes accessed | tf_op | source)
XLA Modules:
  0.0 182.3 jit_solution(1830866541421530069)
XLA Ops:
  0.0 0.5 broadcast.268
  0.5 1.3 reduce.3
  1.9 0.1 squeeze.17
  1.9 0.8 multiply_add_fusion.1
  2.7 0.1 add_add_fusion
  2.8 0.9 convert_reduce_fusion
  3.8 0.1 reduce_sum.12
  3.9 0.7 fusion.9
  4.5 0.1 pad_add_fusion
  4.6 0.6 and_select_fusion.9
  5.2 0.8 convolution_convert_fusion.tab_hbm
  6.1 3.2 %copy.7 = bf16[2,4,8,8,8,256]{5,4,2,3,1,0:T(8,128)(2,1)} copy(bf16[2,4,8,8,8,256]{5,4,3,2,1,0:T(8,128)(2,1)} %bitcast.25) | data formatting | bytes 4194304 | tf_op jit(solution)/shard_map/reshape | solution.py:688
  9.3 163.9 %shard_map.46 = s16[2,8,4,2,96,128]{5,4,3,2,1,0:T(8,128)(2,1)} custom-call(bf16[2,32,64,256]{3,2,1,0:T(8,128)(2,1)} %f2_hbm.1, bf16[64,64,256]{2,1,0:T(8,128)(2,1)} %bitcast.24, s32[8,8,128]{2,1,0:T(8,128)} %convolution_convert_fusion.tab_hbm), custom_call_target="tpu_custom_call" | custom-call | tf_op jit(solution)/shard_map/pallas_call | solution.py:721
  173.2 9.1 %shard_map.47 = f32[5184,128]{1,0:T(8,128)} custom-call(s32[128]{0:T(128)} %get-tuple-element.14.source_ref, s32[128]{0:T(128)} %get-tuple-element.15.half_ref, s16[2,64,96,128]{3,2,1,0:T(8,128)(2,1)} %bitcast.23), custom_call_target="tpu_custom_call" | custom-call | tf_op jit(solution)/shard_map/pallas_call | solution.py:763
  (5 shorter events, 0.0 us)

commit v3 on v2

--- a/solution.py
+++ b/solution.py
@@ -230,7 +230,7 @@
 
 
 MESH = pl.DeviceIdType.MESH
-TOP = 32767.0
+TOP = 32000.0
 
 
 def flipped(index, bit):
@@ -241,10 +241,13 @@
     plan,
     f2_hbm,
     q_hbm,
-    tab_hbm,
+    owner_ref,
+    tile_ref,
     rep_out,
+    idx_out,
     f2x,
     f1a,
+    tab_made,
     tabv,
     tabs,
     map0,
@@ -268,8 +271,10 @@
 ):
     row_count, plane_count, slots, scale = plan
     frame_count, band_rows, band_cols, channels = f2_hbm.shape
-    block_count, block_cells, _ = q_hbm.shape
     side = 2 * RADIUS
+    subs, across = band_rows // side, band_cols // side
+    per_frame = subs * across
+    block_count, block_cells = frame_count * per_frame, side * side
     span = 4 * RADIUS
     wside = 2 * RADIUS + 1
     wide = 2 * side
@@ -339,11 +344,10 @@
         def _():
             halo_copy(b, at, way, False, own).start()
 
-    def f1_copy(index, row, half, bit, own=False):
+    def f1_copy(index, row, half, bit):
         part = pl.ds(half * half_blocks, half_blocks)
-        source = q_hbm.at[part] if own else f1a.at[row, part]
         return pltpu.make_async_remote_copy(
-            src_ref=source,
+            src_ref=f1a.at[row, part],
             dst_ref=f1a.at[row, part],
             send_sem=fs_sem.at[index],
             recv_sem=fr_sem.at[row, half],
@@ -353,7 +357,7 @@
 
     def tab_copy(k):
         return pltpu.make_async_remote_copy(
-            src_ref=tab_hbm.at[(r + k) % row_count],
+            src_ref=tab_made.at[(r + k) % row_count],
             dst_ref=tabv.at[r],
             send_sem=ts_sem.at[k],
             recv_sem=tr_sem.at[k],
@@ -387,12 +391,70 @@
     ]
     f1_third = [(12, d_row, 0, 1), (13, d_row, 1, 1)]
 
+    def whole_part(values, unit):
+        return jnp.floor((values + 0.5) * (1.0 / unit))
+
+    def make_tables():
+        ids = lax.broadcasted_iota(jnp.int32, (block_count, block_count), 0).astype(jnp.float32)
+        lanes = lax.broadcasted_iota(jnp.int32, (block_count, block_count), 1).astype(jnp.float32)
+        block = lanes[:1]
+        spots = lax.broadcasted_iota(
+            jnp.int32, (block_count, tab_made.shape[2]), 1
+        ).astype(jnp.float32)
+        peers = lax.broadcasted_iota(jnp.int32, (row_count, block_count), 0).astype(jnp.float32)
+
+        def upright(line_values):
+            return jnp.sum(jnp.where(ids == lanes, line_values, 0.0), axis=1, keepdims=True)
+
+        tab_made[...] = jnp.zeros(tab_made.shape, tab_made.dtype)
+        idx_out[...] = jnp.zeros(idx_out.shape, idx_out.dtype)
+        totals = [0.0, 0.0, 0.0]
+        for level in range(LEVELS):
+            owner = owner_ref[level].astype(jnp.float32)
+            tile = tile_ref[level : level + 1].astype(jnp.float32)
+            level_across = across >> level
+            tiles = (subs >> level) * level_across
+            tile = tile - whole_part(tile, tiles) * tiles
+            tile_row = whole_part(tile, level_across)
+            same = jnp.where((upright(owner) == owner) & (ids < lanes), 1.0, 0.0)
+            rank = jnp.sum(same, axis=0, keepdims=True)
+            towards = whole_part(owner, plane_count)
+            plane = owner - towards * plane_count
+            place = (plane * LEVELS + level) * slots + rank
+            map_rows = (band_rows >> level) + side
+            values = [
+                block,
+                whole_part(block, per_frame) * map_rows + tile_row * side,
+                tile - tile_row * level_across,
+            ]
+            place = jnp.where(rank < slots, place, -1.0)
+            chosen = jnp.where(upright(place) == spots, 1.0, 0.0).astype(jnp.bfloat16)
+            for at, value in enumerate(values):
+                named = jnp.where(peers == towards, value, 0.0).astype(jnp.bfloat16)
+                totals[at] += jnp.dot(named, chosen, preferred_element_type=jnp.float32)
+            rank = jnp.minimum(rank, slots - 1.0)
+            pair = whole_part(rank, 2)
+            source = (owner * (slots // 2) + pair).astype(jnp.int32)
+            idx_out[level : level + 1, :block_count] = source
+            half = (rank - 2 * pair).astype(jnp.int32)
+            idx_out[LEVELS + level : LEVELS + level + 1, :block_count] = half
+        for at, total in enumerate(totals):
+            total = total.astype(jnp.int32)
+            for peer in range(row_count):
+                tab_made[peer, at : at + 1, :] = total[peer : peer + 1]
+
     loc_f2 = pltpu.make_async_copy(f2_hbm, f2x.at[c, :, pl.ds(side, band_rows)], loc_sem.at[0])
-    loc_q = pltpu.make_async_copy(q_hbm, f1a.at[r], loc_sem.at[1])
-    loc_tab = pltpu.make_async_copy(tab_hbm.at[r], tabv.at[r], loc_sem.at[2])
-    loc_f2.start()
-    loc_q.start()
-    loc_tab.start()
+    loc_tab = pltpu.make_async_copy(tab_made.at[r], tabv.at[r], loc_sem.at[2])
+
+    def loc_q(k):
+        f, at = k // per_frame, k % per_frame
+        cut = q_hbm.at[f, at // across, :, at % across]
+        return pltpu.make_async_copy(cut, f1a.at[r, k], loc_sem.at[1])
+
+    def start_q(k, carry):
+        loc_q(k).start()
+        return carry
+
     for at in range(strips):
 
         @pl.when(c > 0)
@@ -403,12 +465,17 @@
         def _():
             z_copy(c, at, 1, True).start()
 
+    lax.fori_loop(0, block_count, start_q, 0)
+    loc_f2.start()
+    make_tables()
+    pltpu.make_async_copy(f1a.at[r], f1a.at[r], loc_sem.at[1]).wait()
     for item in f1_first:
-        f1_copy(*item, own=True).start()
+        f1_copy(*item).start()
+    for at in range(strips):
+        send_halo(c, at, 0, True)
     for k in range(1, row_count):
         tab_copy(k).start()
-    for at in range(strips):
-        send_halo(c, at, 0, True)
+    loc_tab.start()
 
     @pl.when(r == 0)
     def _():
@@ -482,7 +549,7 @@
     query_row = lane_id % block_cells // side
     query_col = lane_id[0] % side
     is_first = lane_id[0] < block_cells
-    row_id = lax.broadcasted_iota(jnp.int32, line.shape[1:], 0)
+    row_id = lax.broadcasted_iota(jnp.int32, line.shape[2:], 0)
     line[...] = jnp.zeros(line.shape, line.dtype)
 
     def build(b, level):
@@ -516,11 +583,11 @@
         windows, queries = [], []
         for half in range(2):
             at = (b * LEVELS + level) * slots + 2 * pair + half
-            k, row = tabs[s, 0, at], tabs[s, 1, at]
-            cells = from_map[pl.ds(row, span), pl.ds(tabs[s, 2, at], 2)]
+            k, row = jnp.clip(tabs[s, 0, at], 0, block_count - 1), jnp.clip(tabs[s, 1, at], 0, from_map.shape[0] - span)
+            cells = from_map[pl.ds(row, span), pl.ds(jnp.clip(tabs[s, 2, at], 0, from_map.shape[1] - 2), 2)]
             windows.append(cells.reshape(span * span, channels).astype(jnp.bfloat16))
-            queries.append(f1a[s, k])
-        queries = jnp.concatenate(queries, axis=0)
+            queries.append(f1a[s, k].astype(jnp.float32).reshape(block_cells, channels))
+        queries = jnp.concatenate(queries, axis=0).astype(jnp.bfloat16)
         first, second = [
             lax.dot_general(
                 window, queries, (((1,), (1,)), ((), ())), preferred_element_type=jnp.float32
@@ -536,12 +603,11 @@
             flat = jnp.where((query_col & bit) != 0, moved, flat)
         flat = flat * scale
         for a in range(wside):
-            line[pair, a * wside : (a + 1) * wside, :] = flat[a * span : a * span + wside]
-        found = line[pair]
+            line[level, pair, a * wside : (a + 1) * wside, :] = flat[a * span : a * span + wside]
+        found = line[level, pair]
         top = jnp.max(jnp.abs(found), axis=0, keepdims=True)
         power = jnp.maximum(jnp.ceil(jnp.log2(top)), -100.0)
         coded = jnp.floor(found * (TOP * jnp.exp2(-power)) + 0.5)
-        coded = jnp.clip(coded, -TOP, TOP)
         coded = jnp.where(row_id == wside * wside, power, coded)
         reps[b, s, level, pair] = coded.astype(jnp.int32).astype(jnp.int16)
 
@@ -588,7 +654,6 @@
     for k in range(1, row_count):
         tab_copy(k).wait_recv()
     loc_tab.wait()
-    loc_q.wait()
     loc_f2.wait()
     tab_smem = pltpu.make_async_copy(tabv, tabs, tl_sem)
     tab_smem.start()
@@ -652,25 +717,22 @@
         tab_copy(k).wait_send()
 
 
-def join_kernel(pair_count, window_cells, source_ref, half_ref, reply_ref, out_ref):
-    level = pl.program_id(0)
+def join_kernel(group, index_ref, reply_ref, out_ref):
+    window_cells = out_ref.shape[0]
     padded_rows, lanes = reply_ref.shape[-2:]
     is_first = lax.broadcasted_iota(jnp.int32, (padded_rows, lanes), 1) < lanes // 2
-
-    def step(m, carry):
-        at = 2 * (level * pair_count + m)
-        picked = []
-        for side in range(2):
-            rows = reply_ref[0, source_ref[at + side]].astype(jnp.int32).astype(jnp.float32)
-            moved = pltpu.roll(rows, lanes // 2, 1)
-            picked.append(jnp.where(half_ref[at + side] == side, rows, moved))
-        both = jnp.where(is_first, picked[0], picked[1])
-        unit = jnp.exp2(both[window_cells : window_cells + 1]) * (1.0 / TOP)
-        spot = pl.ds(m * LEVELS + level, window_cells, stride=pair_count * LEVELS)
-        out_ref[spot, :] = both[:window_cells] * unit
-        return carry
-
-    lax.fori_loop(0, pair_count, step, 0, unroll=2)
+    base = pl.program_id(0) * group * 2
+    for m in range(group):
+        for level in range(LEVELS):
+            picked = []
+            for side in range(2):
+                at = base + 2 * m + side
+                rows = reply_ref[level, index_ref[level, at]].astype(jnp.int32)
+                turn = (index_ref[LEVELS + level, at] + side) % 2 * (lanes // 2)
+                picked.append(pltpu.roll(rows.astype(jnp.float32), turn, 1))
+            both = jnp.where(is_first, picked[0], picked[1])
+            unit = jnp.exp2(both[window_cells : window_cells + 1]) * (1.0 / TOP)
+            out_ref[:, m * LEVELS + level, :] = both[:window_cells] * unit
 
 
 def gathered_body(fmap1, fmap2, target_owner, target_tile):
@@ -686,48 +748,33 @@
     block_cells = side * side
     slots = max(2, (2 * block_count + device_count - 1) // device_count)
     queries = fmap1.reshape(frame_count, subs, side, across, side, channels)
-    queries = queries.transpose(0, 1, 3, 2, 4, 5).reshape(block_count, block_cells, channels)
-
-    owner = target_owner[:, :, 0]
-    block_ids = jnp.arange(block_count, dtype=jnp.int32)
-    earlier = block_ids[:, None] > block_ids[None, :]
-    same = owner[:, :, None] == owner[:, None, :]
-    rank = jnp.sum((same & earlier).astype(jnp.int32), axis=2)
-    values, places = [], []
-    for level in range(LEVELS):
-        level_across = across >> level
-        tile = target_tile[level] % ((subs >> level) * level_across)
-        map_rows = (band_rows >> level) + side
-        row = block_ids // per_frame * map_rows + tile // level_across * side
-        values.append(jnp.stack([block_ids, row, tile % level_across]))
-        places.append((owner[level] % plane_count * LEVELS + level) * slots + rank[level])
-    values = jnp.pad(jnp.concatenate(values, axis=1), ((0, 5), (0, 0)))
-    places = jnp.concatenate(places)
-    towards = owner.reshape(-1) // plane_count
+    owner = target_owner.transpose(0, 2, 1)
     lanes_used = -(-plane_count * LEVELS * slots // 128) * 128
-    named = towards == jnp.arange(row_count, dtype=jnp.int32)[:, None]
-    left = jnp.where(named[:, None, :], values[None], 0).astype(jnp.float32)
-    right = (places[:, None] == jnp.arange(lanes_used, dtype=jnp.int32)).astype(jnp.float32)
-    table = lax.dot_general(
-        left, right, (((2,), (0,)), ((), ())), precision=lax.Precision.HIGHEST
-    ).astype(jnp.int32)
-
+    table = (row_count, 8, lanes_used)
     padded_rows = -(-(window_cells + 1) // 16) * 16
     pairs = slots // 2
     strips = across // 2
     reply_shape = (LEVELS, row_count, plane_count, pairs, padded_rows, 2 * block_cells)
     ext_rows = band_rows + 2 * side
     dma = pltpu.SemaphoreType.DMA
-    replies = pl.pallas_call(
+    replies, index = pl.pallas_call(
         functools.partial(lookup_kernel, (row_count, plane_count, slots, channels**-0.5)),
-        out_shape=jax.ShapeDtypeStruct(reply_shape, jnp.int16),
-        in_specs=[pl.BlockSpec(memory_space=pl.ANY)] * 3,
-        out_specs=pl.BlockSpec(memory_space=pl.ANY),
+        out_shape=[
+            jax.ShapeDtypeStruct(reply_shape, jnp.int16),
+            jax.ShapeDtypeStruct((8, 128), jnp.int32),
+        ],
+        in_specs=[pl.BlockSpec(memory_space=pl.ANY)] * 2
+        + [pl.BlockSpec(memory_space=pltpu.VMEM)] * 2,
+        out_specs=[
+            pl.BlockSpec(memory_space=pl.ANY),
+            pl.BlockSpec(memory_space=pltpu.VMEM),
+        ],
         scratch_shapes=[
             pltpu.VMEM((plane_count, frame_count, ext_rows, band_cols, channels), jnp.bfloat16),
-            pltpu.VMEM((row_count, block_count, block_cells, channels), jnp.bfloat16),
-            pltpu.VMEM(table.shape, jnp.int32),
-            pltpu.SMEM(table.shape, jnp.int32),
+            pltpu.VMEM((row_count, block_count, side, side, channels), jnp.bfloat16),
+            pltpu.VMEM(table, jnp.int32),
+            pltpu.VMEM(table, jnp.int32),
+            pltpu.SMEM(table, jnp.int32),
             pltpu.VMEM((frame_count * (band_rows + side), across + 1, side, channels), jnp.float32),
             pltpu.VMEM(
                 (frame_count * (band_rows // 2 + side), across // 2 + 1, side, channels),
@@ -737,7 +784,7 @@
                 (plane_count, frame_count, ext_rows // 2, band_cols // 2, channels), jnp.float32
             ),
             pltpu.VMEM((channels // 128, ext_rows // 2 * 2 * side, 128), jnp.float32),
-            pltpu.VMEM((pairs, padded_rows, 2 * block_cells), jnp.float32),
+            pltpu.VMEM((LEVELS, pairs, padded_rows, 2 * block_cells), jnp.float32),
             pltpu.VMEM(
                 (plane_count, row_count, LEVELS, pairs, padded_rows, 2 * block_cells), jnp.int16
             ),
@@ -757,29 +804,23 @@
         compiler_params=pltpu.CompilerParams(
             collective_id=0, has_side_effects=True, vmem_limit_bytes=62 * 2**20
         ),
-    )(fmap2, queries, table)
+    )(fmap2, queries, owner, target_tile)
     spots = row_count * plane_count * pairs
-    source_ids = owner * pairs + rank // 2
+    group = 8 // LEVELS
     joined = pl.pallas_call(
-        functools.partial(join_kernel, block_count // 2, window_cells),
+        functools.partial(join_kernel, group),
         out_shape=jax.ShapeDtypeStruct(
-            (window_cells * block_count // 2 * LEVELS, 2 * block_cells), jnp.float32
+            (window_cells, block_count // 2 * LEVELS, 2 * block_cells), jnp.float32
         ),
-        grid_spec=pltpu.PrefetchScalarGridSpec(
-            num_scalar_prefetch=2,
-            grid=(LEVELS,),
-            in_specs=[
-                pl.BlockSpec((1, spots, padded_rows, 2 * block_cells), lambda l, *_: (l, 0, 0, 0))
-            ],
-            out_specs=pl.BlockSpec(
-                (window_cells * block_count // 2 * LEVELS, 2 * block_cells), lambda l, *_: (0, 0)
-            ),
+        grid=(block_count // 2 // group,),
+        in_specs=[
+            pl.BlockSpec(memory_space=pltpu.SMEM),
+            pl.BlockSpec((LEVELS, spots, padded_rows, 2 * block_cells), lambda g: (0, 0, 0, 0)),
+        ],
+        out_specs=pl.BlockSpec(
+            (window_cells, group * LEVELS, 2 * block_cells), lambda g: (0, g, 0)
         ),
-    )(
-        source_ids.reshape(-1),
-        (rank % 2).reshape(-1),
-        replies.reshape(LEVELS, spots, padded_rows, 2 * block_cells),
-    )
+    )(index, replies.reshape(LEVELS, spots, padded_rows, 2 * block_cells))
     joined = joined.reshape(window_cells, block_count // 2, LEVELS, 2 * block_cells)
     return joined.transpose(2, 0, 1, 3).reshape(LEVELS, window_cells, block_count * block_cells)
 

time: 183 us -> 174 us (0.951)
  other arithmetic: 4.53 us -> 0 us
  local copies, waits for them, and re-layouts: 3.88 us -> 0 us
    reshape x1 -> x0, local copies, waits for them, and re-layouts: 3.19 us -> none  [gathered_body(): queries = fmap1.reshape(frame_count, subs, side, across, side, channels)]
    pallas_call x1, Pallas kernels: 164 us -> 167 us  [gathered_body(): pl.pallas_call(functools.partial(lookup_kernel, (row_count, plane_count,...]
    pallas_call x1, Pallas kernels: 9.07 us -> 6.52 us  [gathered_body(): pl.pallas_call(functools.partial(join_kernel, group), out_shape=jax.Shape...]
where the time goes in v3:
time: 174 us; the launch traced here: 173 us
  Pallas kernels  173 us (99%)
    pallas_call x1, Pallas kernels, gathered_body(): pl.pallas_call(functools.partial(lookup_kernel, (row_count, plane_count,...  167 us
    pallas_call x1, Pallas kernels, gathered_body(): pl.pallas_call(functools.partial(join_kernel, group), out_shape=jax.Shape...  6.52 us

profile of v3, /device:TPU:0, one launch (start us, length us, event | category | flops | bytes accessed | tf_op | source)
XLA Modules:
  0.0 173.0 jit_solution(1145288579190306959)
XLA Ops:
  0.0 166.5 %shard_map.46 = (s16[2,8,4,2,96,128]{5,4,3,2,1,0:T(8,128)(2,1)}, s32[8,128]{1,0:T(8,128)}) custom-call(bf16[2,32,64,256]{3,2,1,0:T(8,128)(2,1)} %f2_hbm.1, bf16[2,4,8,8,8,256]{5,4,3,2,1,0:T(8,128)(2,1)} %bitcast.11, s32[2,1,64]{2,1,0:T(1,128)} %bitcast.12, s32[2,64]{1,0:T(2,128)} %tile_ref.1), custom_call_target="tpu_custom_call" | custom-call | tf_op jit(solution)/shard_map/pallas_call | solution.py:760
  166.5 6.5 %shard_map.47 = f32[81,64,128]{2,1,0:T(8,128)} custom-call(s32[8,128]{1,0:T(8,128)} %get-tuple-element.7.index_ref, s16[2,64,96,128]{3,2,1,0:T(8,128)(2,1)} %bitcast.10), custom_call_target="tpu_custom_call" | custom-call | tf_op jit(solution)/shard_map/pallas_call | solution.py:810

commit v4 on v3

--- a/solution.py
+++ b/solution.py
@@ -303,22 +303,31 @@
     pl.semaphore_wait(barrier, row_count - 1 + has_left + has_right)
 
     def strip(at, way):
-        return at if way == 0 else strips - 1 - at
-
-    def z_copy(b, at, way, own=False):
-        cols = pl.ds(strip(at, way) * wide, wide)
-        here = f2x.at[b, :, pl.ds(side, band_rows), cols]
+        p = at + way * (strips - 1 - 2 * at)
+        return p, pl.ds(pl.multiple_of(p * wide, wide), wide)
+
+    whole_strip = (0, band_rows)
+    last_pieces = [
+        (strips - 1, (0, side)),
+        (strips, (band_rows - side, side)),
+        (strips + 1, (side, band_rows - 2 * side)),
+    ]
+
+    def z_copy(b, number, way, rows=whole_strip, own=False):
+        _, cols = strip(number if rows == whole_strip else strips - 1, way)
+        first, count = rows
+        here = f2x.at[b, :, pl.ds(side + first, count), cols]
         return pltpu.make_async_remote_copy(
-            src_ref=f2_hbm.at[:, :, cols] if own else here,
+            src_ref=f2_hbm.at[:, pl.ds(first, count), cols] if own else here,
             dst_ref=here,
-            send_sem=zs_sem.at[way, b, at],
-            recv_sem=zr_sem.at[b, at],
-            device_id=(r, c - 1 if way == 0 else c + 1),
+            send_sem=zs_sem.at[way, b, number],
+            recv_sem=zr_sem.at[b, number],
+            device_id=(r, c - 1 + 2 * way),
             device_id_type=MESH,
         )
 
     def halo_copy(b, at, way, up, own=False):
-        cols = pl.ds(strip(at, way) * wide, wide)
+        _, cols = strip(at, way)
         first = 0 if up else band_rows - side
         into = band_rows + side if up else 0
         if own:
@@ -335,14 +344,13 @@
             device_id_type=MESH,
         )
 
-    def send_halo(b, at, way, own=False):
-        @pl.when(r > 0)
+    def send_halo(b, at, way, up, own=False):
+        @pl.when(r > 0 if up else r < last_r)
         def _():
-            halo_copy(b, at, way, True, own).start()
-
-        @pl.when(r < last_r)
-        def _():
-            halo_copy(b, at, way, False, own).start()
+            halo_copy(b, at, way, up, own).start()
+
+    def goes_on(way):
+        return (c - 1 + 2 * way >= 0) & (c - 1 + 2 * way <= last_c)
 
     def f1_copy(index, row, half, bit):
         part = pl.ds(half * half_blocks, half_blocks)
@@ -455,15 +463,14 @@
         loc_q(k).start()
         return carry
 
-    for at in range(strips):
-
-        @pl.when(c > 0)
+    for way in range(2):
+
+        @pl.when(goes_on(way))
         def _():
-            z_copy(c, at, 0, True).start()
-
-        @pl.when(c < last_c)
-        def _():
-            z_copy(c, at, 1, True).start()
+            for at in range(strips - 1):
+                z_copy(c, at, way, own=True).start()
+            for number, rows in last_pieces:
+                z_copy(c, number, way, rows, own=True).start()
 
     lax.fori_loop(0, block_count, start_q, 0)
     loc_f2.start()
@@ -472,7 +479,8 @@
     for item in f1_first:
         f1_copy(*item).start()
     for at in range(strips):
-        send_halo(c, at, 0, True)
+        send_halo(c, at, 0, True, own=True)
+        send_halo(c, at, 0, False, own=True)
     for k in range(1, row_count):
         tab_copy(k).start()
     loc_tab.start()
@@ -488,32 +496,54 @@
         )
 
     def each_side(step, act):
-        @pl.when(c + step <= last_c)
-        def _():
-            act(c + step, 0)
-
-        if step > 0:
-
-            @pl.when(c - step >= 0)
+        def one(way, carry):
+            b = c + step * (1 - 2 * way)
+
+            @pl.when((b >= 0) & (b <= last_c))
             def _():
-                act(c - step, 1)
+                act(b, way)
+
+            return carry
+
+        lax.fori_loop(0, jnp.where(step > 0, 2, 1), one, 0)
 
     def take(step, at):
         def act(b, way):
             z_copy(b, at, way).wait_recv()
 
-            @pl.when(c > 0 if way == 0 else c < last_c)
+            @pl.when(goes_on(way))
             def _():
                 z_copy(b, at, way).start()
 
-            send_halo(b, at, way)
+            send_halo(b, at, way, True)
+            send_halo(b, at, way, False)
 
         each_side(step, act)
 
-    def pool(step, ats):
+    def take_last(step):
         def act(b, way):
-            for at in ats:
-
+            for place, (number, rows) in enumerate(last_pieces):
+                z_copy(b, number, way, rows).wait_recv()
+
+                @pl.when(goes_on(way))
+                def _():
+                    z_copy(b, number, way, rows).start()
+
+                if place < 2:
+                    send_halo(b, strips - 1, way, place == 0)
+
+        each_side(step, act)
+
+    def take_some(step, low, high):
+        def one(at, carry):
+            take(step, at)
+            return carry
+
+        lax.fori_loop(low, high, one, 0)
+
+    def pool(step, low, high):
+        def act(b, way):
+            def strip_pool(at, carry):
                 @pl.when(r > 0)
                 def _():
                     halo_copy(b, at, way, False).wait_recv()
@@ -522,26 +552,26 @@
                 def _():
                     halo_copy(b, at, way, True).wait_recv()
 
-            rows = p1x.shape[2]
-            for at in ats:
-                col = strip(at, way)
-
-                def pool_row(t, carry):
+                rows = p1x.shape[2]
+                p, cols = strip(at, way)
+                half_cols = pl.ds(pl.multiple_of(p * side, side), side)
+
+                def pool_row(t, inner):
                     f, i = t // rows, t % rows
-                    pair = f2x[b, f, pl.ds(2 * i, 2), col * wide : (col + 1) * wide]
-                    pair = pair.astype(jnp.float32)
+                    pair = f2x[b, f, pl.ds(2 * i, 2), cols].astype(jnp.float32)
                     both = pair[0] + pair[1]
                     for lane in range(channels // 128):
                         tmp[lane, pl.ds(i * wide, wide), :] = both[:, lane * 128 : (lane + 1) * 128]
                     for lane in range(channels // 128):
                         even = tmp[lane, pl.ds(i * wide, side, stride=2), :]
                         odd = tmp[lane, pl.ds(i * wide + 1, side, stride=2), :]
-                        p1x[
-                            b, f, i, col * side : (col + 1) * side, lane * 128 : (lane + 1) * 128
-                        ] = (even + odd) * 0.25
-                    return carry
+                        p1x[b, f, i, half_cols, lane * 128 : (lane + 1) * 128] = (even + odd) * 0.25
+                    return inner
 
                 lax.fori_loop(0, frame_count * rows, pool_row, 0, unroll=4)
+                return carry
+
+            lax.fori_loop(low, high, strip_pool, 0)
 
         each_side(step, act)
 
@@ -576,7 +606,7 @@
             into[t] = whole[: width + side].reshape(into.shape[1:])
             return carry
 
-        lax.fori_loop(0, into.shape[0], build_row, 0)
+        lax.fori_loop(0, into.shape[0], build_row, 0, unroll=4)
 
     def score_pair(b, s, level, pair):
         from_map = (map0, map1)[level]
@@ -633,15 +663,15 @@
 
         lax.fori_loop(0, row_count, source, 0)
 
-    for at in range(strips):
-        take(1, at)
+    take_some(1, 0, strips - 1)
+    take_last(1)
     for item in f1_second:
         index, row, half, bit = item
         if index in (6, 7, 9, 10):
             f1_copy(*item).wait_recv()
         f1_copy(*item).start()
-    for at in range(strips - 1):
-        take(2, at)
+    if last_c >= 2:
+        take_some(2, 0, strips - 1)
     for item in f1_third:
         f1_copy(*item).wait_recv()
         f1_copy(*item).start()
@@ -658,46 +688,53 @@
     tab_smem = pltpu.make_async_copy(tabv, tabs, tl_sem)
     tab_smem.start()
     tab_smem.wait()
-    near, rest = [0], list(range(1, strips))
-    pool(0, near + rest)
-    pool(1, near)
-    each_side(0, process)
-    take(2, strips - 1)
-    for step in range(1, plane_count):
-        if step > 2:
-            for at in rest:
-                take(step, at)
-        if step >= 2 and step + 1 < plane_count:
+    def stage(step, carry):
+        @pl.when(step == 1)
+        def _():
+            take_last(jnp.int32(2))
+
+        @pl.when(step > 2)
+        def _():
+            take_some(step, 1, strips - 1)
+            take_last(step)
+
+        @pl.when(step >= 2)
+        def _():
             take(step + 1, 0)
-        pool(step, rest)
-        if step + 1 < plane_count:
-            pool(step + 1, near)
+
+        pool(step, jnp.where(step == 0, 0, 1), strips)
+        pool(step + 1, 0, 1)
         each_side(step, process)
-
-    for at in range(strips):
-
-        @pl.when(c < last_c)
+        return carry
+
+    lax.fori_loop(0, last_c + 1, stage, 0)
+
+    def all_sent(b, way):
+        @pl.when(goes_on(way))
         def _():
-            z_copy(c, at, 1).wait_send()
-
-    for step in range(plane_count):
-
-        def sent(b, way):
-            for at in range(strips):
-
-                @pl.when(c > 0 if way == 0 else c < last_c)
-                def _():
-                    z_copy(b, at, way).wait_send()
-
-                @pl.when(r > 0)
-                def _():
-                    halo_copy(b, at, way, True).wait_send()
-
-                @pl.when(r < last_r)
-                def _():
-                    halo_copy(b, at, way, False).wait_send()
-
-        each_side(step, sent)
+            for at in range(strips - 1):
+                z_copy(b, at, way).wait_send()
+            for number, rows in last_pieces:
+                z_copy(b, number, way, rows).wait_send()
+
+    def halos_sent(b, way):
+        for at in range(strips):
+
+            @pl.when(r > 0)
+            def _():
+                halo_copy(b, at, way, True).wait_send()
+
+            @pl.when(r < last_r)
+            def _():
+                halo_copy(b, at, way, False).wait_send()
+
+    def step_sent(step, carry):
+        each_side(step, all_sent)
+        each_side(step, halos_sent)
+        return carry
+
+    all_sent(c, 1)
+    lax.fori_loop(0, last_c + 1, step_sent, 0)
 
     def plane_end(b, carry):
         rep_local(b).wait()
@@ -751,7 +788,7 @@
     owner = target_owner.transpose(0, 2, 1)
     lanes_used = -(-plane_count * LEVELS * slots // 128) * 128
     table = (row_count, 8, lanes_used)
-    padded_rows = -(-(window_cells + 1) // 16) * 16
+    padded_rows = -(-(window_cells + 1) // 8) * 8
     pairs = slots // 2
     strips = across // 2
     reply_shape = (LEVELS, row_count, plane_count, pairs, padded_rows, 2 * block_cells)
@@ -789,8 +826,8 @@
                 (plane_count, row_count, LEVELS, pairs, padded_rows, 2 * block_cells), jnp.int16
             ),
             dma((3,)),
-            dma((2, plane_count, strips)),
-            dma((plane_count, strips)),
+            dma((2, plane_count, strips + 2)),
+            dma((plane_count, strips + 2)),
             dma((2, plane_count, strips)),
             dma((2, plane_count, strips)),
             dma((14,)),

time: 174 us -> 169 us (0.971)
  Pallas kernels: 173 us -> 168 us
    pallas_call x1, Pallas kernels: 167 us -> 161 us  [gathered_body(): pl.pallas_call(functools.partial(lookup_kernel, (row_count, plane_count,...]
where the time goes in v4:
time: 169 us; the launch traced here: 168 us
  Pallas kernels  168 us (99%)
    pallas_call x1, Pallas kernels, gathered_body(): pl.pallas_call(functools.partial(lookup_kernel, (row_count, plane_count,...  161 us
    pallas_call x1, Pallas kernels, gathered_body(): pl.pallas_call(functools.partial(join_kernel, group), out_shape=jax.Shape...  6.45 us

profile of v4, /device:TPU:0, one launch (start us, length us, event | category | flops | bytes accessed | tf_op | source)
XLA Modules:
  0.0 167.9 jit_solution(17525323277185614332)
XLA Ops:
  0.0 161.4 %shard_map.46 = (s16[2,8,4,2,88,128]{5,4,3,2,1,0:T(8,128)(2,1)}, s32[8,128]{1,0:T(8,128)}) custom-call(bf16[2,32,64,256]{3,2,1,0:T(8,128)(2,1)} %f2_hbm.1, bf16[2,4,8,8,8,256]{5,4,3,2,1,0:T(8,128)(2,1)} %bitcast.11, s32[2,1,64]{2,1,0:T(1,128)} %bitcast.12, s32[2,64]{1,0:T(2,128)} %tile_ref.1), custom_call_target="tpu_custom_call" | custom-call | tf_op jit(solution)/shard_map/pallas_call | solution.py:797
  161.4 6.4 %shard_map.47 = f32[81,64,128]{2,1,0:T(8,128)} custom-call(s32[8,128]{1,0:T(8,128)} %get-tuple-element.7.index_ref, s16[2,64,88,128]{3,2,1,0:T(8,128)(2,1)} %bitcast.10), custom_call_target="tpu_custom_call" | custom-call | tf_op jit(solution)/shard_map/pallas_call | solution.py:847

commit v5 on v4

--- a/solution.py
+++ b/solution.py
@@ -507,7 +507,7 @@
 
         lax.fori_loop(0, jnp.where(step > 0, 2, 1), one, 0)
 
-    def take(step, at):
+    def take(step, at, halo=True):
         def act(b, way):
             z_copy(b, at, way).wait_recv()
 
@@ -515,12 +515,13 @@
             def _():
                 z_copy(b, at, way).start()
 
-            send_halo(b, at, way, True)
-            send_halo(b, at, way, False)
+            if halo:
+                send_halo(b, at, way, True)
+                send_halo(b, at, way, False)
 
         each_side(step, act)
 
-    def take_last(step):
+    def take_last(step, halo=True):
         def act(b, way):
             for place, (number, rows) in enumerate(last_pieces):
                 z_copy(b, number, way, rows).wait_recv()
@@ -529,14 +530,14 @@
                 def _():
                     z_copy(b, number, way, rows).start()
 
-                if place < 2:
+                if halo and place < 2:
                     send_halo(b, strips - 1, way, place == 0)
 
         each_side(step, act)
 
-    def take_some(step, low, high):
+    def take_some(step, low, high, halo=True):
         def one(at, carry):
-            take(step, at)
+            take(step, at, halo)
             return carry
 
         lax.fori_loop(low, high, one, 0)
@@ -616,8 +617,8 @@
             k, row = jnp.clip(tabs[s, 0, at], 0, block_count - 1), jnp.clip(tabs[s, 1, at], 0, from_map.shape[0] - span)
             cells = from_map[pl.ds(row, span), pl.ds(jnp.clip(tabs[s, 2, at], 0, from_map.shape[1] - 2), 2)]
             windows.append(cells.reshape(span * span, channels).astype(jnp.bfloat16))
-            queries.append(f1a[s, k].astype(jnp.float32).reshape(block_cells, channels))
-        queries = jnp.concatenate(queries, axis=0).astype(jnp.bfloat16)
+            queries.append(f1a[s, k].reshape(block_cells, channels))
+        queries = jnp.concatenate(queries, axis=0)
         first, second = [
             lax.dot_general(
                 window, queries, (((1,), (1,)), ((), ())), preferred_element_type=jnp.float32
@@ -645,8 +646,12 @@
         for level in range(LEVELS):
             build(b, level)
 
-        def source(k, inner):
-            s = (r + k) % row_count
+        def source(j, inner):
+            flips = (1 - j // 4, (j // 2 + j // 4) % 2, (j + j // 6) % 2)
+            s = r
+            for flip, bit in zip(flips, (2, 4, 1), strict=True):
+                s = s + flip * (bit - 2 * bit * (r // bit % 2))
+            k = (s - r + row_count) % row_count
             for level in range(LEVELS):
                 for pair in range(slots // 2):
                     score_pair(b, s, level, pair)
@@ -663,13 +668,23 @@
 
         lax.fori_loop(0, row_count, source, 0)
 
-    take_some(1, 0, strips - 1)
-    take_last(1)
+    take_some(1, 0, strips - 1, False)
+    take_last(1, False)
     for item in f1_second:
         index, row, half, bit = item
         if index in (6, 7, 9, 10):
             f1_copy(*item).wait_recv()
         f1_copy(*item).start()
+
+    def first_halos(at, carry):
+        def act(b, way):
+            send_halo(b, at, way, True)
+            send_halo(b, at, way, False)
+
+        each_side(1, act)
+        return carry
+
+    lax.fori_loop(0, strips, first_halos, 0)
     if last_c >= 2:
         take_some(2, 0, strips - 1)
     for item in f1_third:

time: 169 us -> 166 us (0.982)
  Pallas kernels: 168 us -> 166 us
    pallas_call x1, Pallas kernels: 161 us -> 159 us  [gathered_body(): pl.pallas_call(functools.partial(lookup_kernel, (row_count, plane_count,...]
where the time goes in v5:
time: 166 us
  Pallas kernels  166 us (100%)
    pallas_call x1, Pallas kernels, gathered_body(): pl.pallas_call(functools.partial(lookup_kernel, (row_count, plane_count,...  159 us
    pallas_call x1, Pallas kernels, gathered_body(): pl.pallas_call(functools.partial(join_kernel, group), out_shape=jax.Shape...  6.45 us

profile of v5, /device:TPU:0, one launch (start us, length us, event | category | flops | bytes accessed | tf_op | source)
XLA Modules:
  0.0 165.6 jit_solution(9801659353039470653)
XLA Ops:
  0.0 159.1 %shard_map.46 = (s16[2,8,4,2,88,128]{5,4,3,2,1,0:T(8,128)(2,1)}, s32[8,128]{1,0:T(8,128)}) custom-call(bf16[2,32,64,256]{3,2,1,0:T(8,128)(2,1)} %f2_hbm.1, bf16[2,4,8,8,8,256]{5,4,3,2,1,0:T(8,128)(2,1)} %bitcast.11, s32[2,1,64]{2,1,0:T(1,128)} %bitcast.12, s32[2,64]{1,0:T(2,128)} %tile_ref.1), custom_call_target="tpu_custom_call" | custom-call | tf_op jit(solution)/shard_map/pallas_call | solution.py:812
  159.1 6.4 %shard_map.47 = f32[81,64,128]{2,1,0:T(8,128)} custom-call(s32[8,128]{1,0:T(8,128)} %get-tuple-element.7.index_ref, s16[2,64,88,128]{3,2,1,0:T(8,128)(2,1)} %bitcast.10), custom_call_target="tpu_custom_call" | custom-call | tf_op jit(solution)/shard_map/pallas_call | solution.py:862

commit v6 on v5

--- a/solution.py
+++ b/solution.py
@@ -711,13 +711,15 @@
         @pl.when(step > 2)
         def _():
             take_some(step, 1, strips - 1)
+            pool(step, 1, strips - 1)
             take_last(step)
 
         @pl.when(step >= 2)
         def _():
             take(step + 1, 0)
 
-        pool(step, jnp.where(step == 0, 0, 1), strips)
+        low = jnp.where(step == 0, 0, jnp.where(step > 2, strips - 1, 1))
+        pool(step, low, strips)
         pool(step + 1, 0, 1)
         each_side(step, process)
         return carry

time: 166 us -> 166 us (level)
  no operation moved by 1% of the time
where the time goes in v6:
time: 166 us; the launch traced here: 165 us
  Pallas kernels  165 us (99%)
    pallas_call x1, Pallas kernels, gathered_body(): pl.pallas_call(functools.partial(lookup_kernel, (row_count, plane_count,...  159 us
    pallas_call x1, Pallas kernels, gathered_body(): pl.pallas_call(functools.partial(join_kernel, group), out_shape=jax.Shape...  6.45 us

profile of v6, /device:TPU:0, one launch (start us, length us, event | category | flops | bytes accessed | tf_op | source)
XLA Modules:
  0.0 165.4 jit_solution(13877802040323634585)
XLA Ops:
  0.0 158.9 %shard_map.46 = (s16[2,8,4,2,88,128]{5,4,3,2,1,0:T(8,128)(2,1)}, s32[8,128]{1,0:T(8,128)}) custom-call(bf16[2,32,64,256]{3,2,1,0:T(8,128)(2,1)} %f2_hbm.1, bf16[2,4,8,8,8,256]{5,4,3,2,1,0:T(8,128)(2,1)} %bitcast.11, s32[2,1,64]{2,1,0:T(1,128)} %bitcast.12, s32[2,64]{1,0:T(2,128)} %tile_ref.1), custom_call_target="tpu_custom_call" | custom-call | tf_op jit(solution)/shard_map/pallas_call | solution.py:814
  158.9 6.4 %shard_map.47 = f32[81,64,128]{2,1,0:T(8,128)} custom-call(s32[8,128]{1,0:T(8,128)} %get-tuple-element.7.index_ref, s16[2,64,88,128]{3,2,1,0:T(8,128)(2,1)} %bitcast.10), custom_call_target="tpu_custom_call" | custom-call | tf_op jit(solution)/shard_map/pallas_call | solution.py:864
